TPU v7x, 8 devices: a whole 2x2x1 slice. The times are simulated.
8 devices in a mesh: dp: 1 (over z), ep: 8 (over y, x, core).
Axes of the slice: x: 2, y: 2, z: 1, core: 2. Of those that a mesh axis runs over, the one named last changes fastest.
Arguments:
- hidden: bfloat16 [16384, 2048], P(('dp', 'ep'))
- w_router: bfloat16 [2048, 64], replicated
- w_gate: bfloat16 [64, 2048, 1408], P('ep')
- w_up: bfloat16 [64, 2048, 1408], P('ep')
- w_down: bfloat16 [64, 1408, 2048], P('ep')
- shared_gate: bfloat16 [2048, 2816], replicated
- shared_up: bfloat16 [2048, 2816], replicated
- shared_down: bfloat16 [2816, 2048], replicated
- top_idx: int32 [16384, 6], P(('dp', 'ep'))
- keep_mask: int32 [16384, 6], P(('dp', 'ep'))
Outputs:
- output: bfloat16 [16384, 2048], P(('dp', 'ep'))
All inputs are finite; a program needn't handle non-finite values.
Results may differ from a plain program's by a relative error of at most 0.00689379.
Values are sent between devices in bfloat16 or wider.
A program may use at most 1 GiB of HBM per device.

v0:
```python
import jax
import jax.numpy as jnp
from jax import lax
from jax.experimental import pallas as pl
from jax.experimental.pallas import tpu as pltpu
from jax.sharding import PartitionSpec as P

ROUTE_SCALE = 16.0
CAP = 384
LANES = 128
STRIDE = CAP + 8
SIZES = (64, 128, 192, 256, 320, 384)
UNROLL = 16
BATCH = 8


def swiglu(tok_rows, gate_w, up_w, down_w):
    h_gate = jnp.dot(tok_rows, gate_w, preferred_element_type=jnp.float32)
    h_up = jnp.dot(tok_rows, up_w, preferred_element_type=jnp.float32)
    act_rows = (jax.nn.silu(h_gate) * h_up).astype(jnp.bfloat16)
    return jnp.dot(act_rows, down_w, preferred_element_type=jnp.float32)


def bank_kernel(tok, gate, cnt, xa_hbm, xb_hbm, w1a, w3a, w2a, w1b, w3b, w2b, out_hbm,
                x_v, acc, w1v, w3v, w2v, xf, xs, hv, stage, x_sem, w1_sem, w3_sem, w2_sem, out_sem):
    tokens, chunks, _ = x_v.shape
    width = chunks * LANES
    per_dev = w1a.shape[0]
    ff = w1a.shape[2]
    experts = 2 * per_dev

    def copy_w(dst, sem, a, b, e, start):
        @pl.when((e < per_dev) & (cnt[e] > 0))
        def _():
            c = pltpu.make_async_copy(a.at[jnp.minimum(e, per_dev - 1)], dst, sem)
            c.start() if start else c.wait()

        @pl.when((e >= per_dev) & (cnt[e] > 0))
        def _():
            c = pltpu.make_async_copy(b.at[jnp.maximum(e - per_dev, 0)], dst, sem)
            c.start() if start else c.wait()

    def in_copies(e, slot, start):
        copy_w(w1v.at[slot], w1_sem.at[slot], w1a, w1b, e, start)
        copy_w(w3v.at[slot], w3_sem.at[slot], w3a, w3b, e, start)

    half = tokens // 2
    x_copies = [pltpu.make_async_copy(src, x_v.at[pl.ds(i * half, half)], x_sem.at[i]) for i, src in enumerate((xa_hbm, xb_hbm))]
    for c in x_copies:
        c.start()
    in_copies(jnp.int32(0), 0, True)
    copy_w(w2v, w2_sem, w2a, w2b, jnp.int32(0), True)

    rows0 = acc.shape[0]
    zblk = 256

    @pl.loop(0, rows0 // zblk)
    def _(i):
        acc[pl.ds(pl.multiple_of(i * zblk, zblk), zblk), :] = jnp.zeros((zblk, LANES), jnp.float32)

    for c in x_copies:
        c.wait()

    def ffn(m, slot):
        for j in range(chunks):
            xs[0:m, j * LANES:(j + 1) * LANES] = xf[j * STRIDE:j * STRIDE + m, :].astype(jnp.bfloat16)

        def gate_up(c0, cw):
            xv = xs[0:m, :]
            g = jnp.dot(xv, w1v[slot, :, c0:c0 + cw], preferred_element_type=jnp.float32)
            u = jnp.dot(xv, w3v[slot, :, c0:c0 + cw], preferred_element_type=jnp.float32)
            hv[0:m, c0:c0 + cw] = (jax.nn.silu(g) * u).astype(jnp.bfloat16)

        for c0 in range(0, ff, 768):
            gate_up(c0, min(768, ff - c0))

    def down(m):
        cols = 1024

        @pl.loop(0, width // cols)
        def _(c):
            o = jnp.dot(hv[0:m, :], w2v[:, pl.ds(pl.multiple_of(c * cols, cols), cols)], preferred_element_type=jnp.float32)
            o = o.astype(jnp.bfloat16).astype(jnp.float32)
            base = pl.multiple_of(c * (cols // LANES * STRIDE), 8)
            for j in range(cols // LANES):
                xf[pl.ds(base + j * STRIDE, m), :] = o[:, j * LANES:(j + 1) * LANES]

    @pl.loop(0, experts)
    def _(e):
        slot = lax.rem(e, 2)
        n = cnt[e]

        @pl.when(e + 1 < experts)
        def _():
            in_copies(e + 1, 1 - slot, True)

        @pl.loop(0, (n + UNROLL - 1) // UNROLL)
        def _(g):
            s0 = pl.multiple_of(g * UNROLL, UNROLL)
            for i in range(UNROLL):
                t = jnp.minimum(tok[e, s0 + i], tokens - 1)
                xf[pl.ds(s0 + i, chunks, stride=STRIDE), :] = x_v[t].astype(jnp.float32)

        in_copies(e, slot, False)
        lo = 0
        for m in SIZES:
            @pl.when((n > lo) & (n <= m))
            def _(m=m):
                ffn(m, slot)

            lo = m

        copy_w(w2v, w2_sem, w2a, w2b, e, False)
        lo = 0
        for m in SIZES:
            @pl.when((n > lo) & (n <= m))
            def _(m=m):
                down(m)

            lo = m

        @pl.when(e + 1 < experts)
        def _():
            copy_w(w2v, w2_sem, w2a, w2b, e + 1, True)

        @pl.loop(0, (n + UNROLL - 1) // UNROLL)
        def _(g):
            s0 = pl.multiple_of(g * UNROLL, UNROLL)
            for first in range(0, UNROLL, BATCH):
                sums = []
                for i in range(first, first + BATCH):
                    base = pl.multiple_of(tok[e, s0 + i] * chunks, chunks)
                    row = xf[pl.ds(s0 + i, chunks, stride=STRIDE), :]
                    sums.append((base, acc[pl.ds(base, chunks), :] + gate[e, s0 + i] * row))
                for base, val in sums:
                    acc[pl.ds(base, chunks), :] = val

    blk = stage.shape[1]
    n_out = tokens // blk

    @pl.loop(0, n_out)
    def _(i):
        slot = lax.rem(i, 2)
        rows = pl.ds(pl.multiple_of(i * blk, blk), blk)

        @pl.when(i >= 2)
        def _():
            pltpu.make_async_copy(stage.at[slot], out_hbm.at[rows], out_sem.at[slot]).wait()

        for j in range(chunks):
            v = acc[pl.ds(i * (blk * chunks) + j, blk, stride=chunks), :]
            stage[slot, :, j * LANES:(j + 1) * LANES] = v.astype(stage.dtype)
        pltpu.make_async_copy(stage.at[slot], out_hbm.at[rows], out_sem.at[slot]).start()

    for i in range(max(0, n_out - 2), n_out):
        pltpu.make_async_copy(stage.at[i % 2], out_hbm.at[pl.ds(i * blk, blk)], out_sem.at[i % 2]).wait()


def expert_bank(tok, gate, cnt, x3, w_own, w_peer, out_dtype):
    half, chunks, _ = x3[0].shape
    tokens = 2 * half
    per_dev, width, ff = w_own[0].shape
    blk = 128
    anys = pl.BlockSpec(memory_space=pl.ANY)
    smem = pl.BlockSpec(memory_space=pltpu.SMEM)
    flops = 2 * per_dev * 200 * 6 * width * ff
    return pl.pallas_call(
        bank_kernel,
        out_shape=jax.ShapeDtypeStruct((tokens, width), out_dtype),
        in_specs=[smem] * 3 + [anys] * 8,
        out_specs=anys,
        scratch_shapes=[
            pltpu.VMEM((tokens, chunks, LANES), jnp.bfloat16),
            pltpu.VMEM(((tokens + 16) * chunks, LANES), jnp.float32),
            pltpu.VMEM((2, width, ff), jnp.bfloat16),
            pltpu.VMEM((2, width, ff), jnp.bfloat16),
            pltpu.VMEM((ff, width), jnp.bfloat16),
            pltpu.VMEM((chunks * STRIDE, LANES), jnp.float32),
            pltpu.VMEM((CAP, width), jnp.bfloat16),
            pltpu.VMEM((CAP, ff), jnp.bfloat16),
            pltpu.VMEM((2, blk, width), out_dtype),
            pltpu.SemaphoreType.DMA((2,)),
            pltpu.SemaphoreType.DMA((2,)),
            pltpu.SemaphoreType.DMA((2,)),
            pltpu.SemaphoreType.DMA,
            pltpu.SemaphoreType.DMA((2,)),
        ],
        compiler_params=pltpu.CompilerParams(vmem_limit_bytes=66_000_000),
        cost_estimate=pl.CostEstimate(flops=flops, bytes_accessed=6 * per_dev * width * ff * 2, transcendentals=0),
    )(tok, gate, cnt, *x3, *w_own, *w_peer)


def solution(mesh):
    groups = mesh.shape["ep"]
    tok_spec = P(("dp", "ep"), None)
    bank_spec = P("ep", None, None)

    def swap(a, s):
        return lax.ppermute(a, "ep", [(i, i ^ s) for i in range(groups)])

    def device_fn(hidden, w_router, w_gate, w_up, w_down, shared_gate, shared_up, shared_down, top_idx, keep_mask):
        tokens, _ = top_idx.shape
        width = hidden.shape[1]
        experts = w_router.shape[1]
        per_chip = 2 * w_gate.shape[0]
        me = lax.axis_index("ep")
        rows = tokens // 2
        x0 = tuple(hidden[i * rows:(i + 1) * rows].reshape(rows, width // LANES, LANES) for i in range(2))
        x2, x4 = (tuple(swap(h, s) for h in x0) for s in (2, 4))
        w_own = (w_gate, w_up, w_down)
        w_peer = tuple(swap(w, 1) for w in w_own)

        logits = jnp.dot(hidden, w_router, preferred_element_type=jnp.float32)
        prob = ROUTE_SCALE * jax.nn.softmax(logits, axis=-1)
        kept_id = jnp.where(keep_mask > 0, top_idx, experts)
        member = jnp.any(kept_id[:, :, None] == jnp.arange(experts)[None, None, :], axis=1)
        member_b = member.astype(jnp.bfloat16)
        t_ids = jnp.arange(tokens, dtype=jnp.int32)
        before = (t_ids[:, None] > t_ids[None, :]).astype(jnp.bfloat16)
        rank = jnp.dot(before, member_b, preferred_element_type=jnp.float32).astype(jnp.int32)
        rank = jnp.where(member, rank, -1)
        hit = rank[:, :, None] == jnp.arange(CAP, dtype=jnp.int32)[None, None, :]
        slot_tok = jnp.min(jnp.where(hit, t_ids[:, None, None].astype(jnp.float32), float(tokens)), axis=0)
        slot_gate = jnp.sum(jnp.where(hit, prob[:, :, None], 0.0), axis=0)
        lists = jnp.stack([slot_tok, slot_gate], axis=1)

        def lists_of(dev):
            return lax.dynamic_slice_in_dim(lists, (dev // 2) * per_chip, per_chip, axis=0)

        def run(x3, lst, out_dtype):
            own_first = lax.rem(me, 2) == 0
            half = per_chip // 2
            lst = jnp.where(own_first, lst, jnp.concatenate([lst[half:], lst[:half]], axis=0))
            tok = lst[:, 0].astype(jnp.int32)
            cnt = jnp.sum((tok < tokens).astype(jnp.int32), axis=1)
            return expert_bank(tok, lst[:, 1], cnt, x3, w_own, w_peer, out_dtype)

        l_in = {s: swap(lists_of(me ^ s), s) for s in (2, 4, 6)}
        shared = swiglu(hidden, shared_gate, shared_up, shared_down)
        x2, x4, shared, l_in = lax.optimization_barrier((x2, x4, shared, l_in))
        x6 = swap(x4[0], 2), swap(x2[1], 4)
        part2 = run(x2, l_in[2], jnp.bfloat16)
        part4 = run(x4, l_in[4], jnp.bfloat16)
        back2, back4 = swap(part2, 2), swap(part4, 4)
        x6, part4 = lax.optimization_barrier((x6, part4))
        back6 = swap(run(x6, l_in[6], jnp.bfloat16), 6)
        total = shared + run(x0, lists_of(me), jnp.float32)
        for b in (back2, back4, back6):
            total = total + b.astype(jnp.float32)
        return total.astype(jnp.bfloat16)

    return jax.shard_map(device_fn, mesh=mesh, in_specs=(tok_spec, P(), bank_spec, bank_spec, bank_spec, P(), P(), P(), tok_spec, tok_spec), out_specs=tok_spec, check_vma=False)
```

profile of v0, /device:TPU:4, one launch (start us, length us, event | category | flops | bytes accessed | tf_op | source)
XLA Modules:
  0.0 923.9 jit_solution(6296620523263816232)
XLA Ops:
  0.0 0.5 collective-permute-start.8
  0.5 0.9 compare_select_fusion
  1.4 0.5 fusion.2
  1.9 1.7 fusion.4
  3.6 0.3 copy.14
  3.9 6.0 fusion.19
  10.0 0.1 fusion.5
  10.1 0.1 divide_multiply_fusion
  10.2 0.3 copy.15
  10.6 41.9 %select_reduce_fusion = (f32[64,384]{1,0:T(8,128)S(1)}, f32[64,384]{1,0:T(8,128)S(1)}) fusion(f32[2048,64]{1,0:T(8,128)S(1)} %copy.15, s32[2048,64]{1,0:T(8,128)S(1)} %copy.14, f32[2048]{0:T(1024)S(1)} %iota_convert_fusion), kind=kLoop, calls=%fused_computation | loop fusion | flops 251609088 | bytes 1253376 | tf_op jit(solution)/shard_map/reduce_sum | solution.py:224
  52.5 0.6 fusion.6
  53.1 1.5 collective-permute-start.4
  54.6 0.5 collective-permute-start.5
  55.1 32.2 %fusion.20 = f32[2048,2816]{1,0:T(8,128)} fusion(bf16[2048,2048]{1,0:T(8,128)(2,1)} %param.10, bf16[2048,2816]{1,0:T(8,128)(2,1)} %param.15), kind=kOutput, calls=%fused_computation.57 | convolution fusion | flops 23622320128 | bytes 42991616 | tf_op jit(solution)/shard_map/dot_general | solution.py:18
  87.3 0.6 copy-done.9
  87.9 1.6 collective-permute-start.6
  89.5 3.7 slice_bitcast_fusion
  93.2 3.6 copy.17
  96.8 7.1 copy.16
  103.9 0.3 collective-permute-start.2
  104.3 1.5 collective-permute-start
  105.8 34.6 %multiply_convert_fusion.clone.4 = bf16[2048,2816]{1,0:T(8,128)(2,1)} fusion(f32[2048,2816]{1,0:T(8,128)} %fusion.20, bf16[2048,2048]{1,0:T(8,128)(2,1)} %param.10, bf16[2048,2816]{1,0:T(8,128)(2,1)} %param.16), kind=kOutput, calls=%fused_computation.3.clone.clone.clone.1 | convolution fusion | flops 23656923136 | bytes 54525952 | tf_op jit(solution)/shard_map/dot_general | solution.py:19
  140.4 56.2 %collective-permute-done.2.xa_hbm = bf16[1024,16,128]{2,1,0:T(8,128)(2,1)} collective-permute-done((bf16[1024,16,128]{2,1,0:T(8,128)(2,1)}, bf16[1024,16,128]{2,1,0:T(8,128)(2,1)}, u32[]{:S(2)}, u32[]{:S(2)}) %collective-permute-start.2) | collective-permute-done | bytes 4194336 | tf_op jit(solution)/shard_map/ppermute | solution.py:199
  196.6 0.3 collective-permute-start.3
  196.9 1.4 collective-permute-start.1
  198.3 31.8 %fusion.1 = f32[2048,2048]{1,0:T(8,128)} fusion(bf16[2816,2048]{1,0:T(8,128)(2,1)} %param.17, bf16[2048,2816]{1,0:T(8,128)(2,1)} %multiply_convert_fusion.clone.4), kind=kOutput, calls=%fused_computation.7 | convolution fusion | flops 23622320128 | bytes 39845888 | tf_op jit(solution)/shard_map/dot_general | solution.py:21
  230.2 58.0 %collective-permute-done.3.xb_hbm = bf16[1024,16,128]{2,1,0:T(8,128)(2,1)S(1)} collective-permute-done((bf16[1024,16,128]{2,1,0:T(8,128)(2,1)S(1)}, bf16[1024,16,128]{2,1,0:T(8,128)(2,1)S(1)}, u32[]{:S(2)}, u32[]{:S(2)}) %collective-permute-start.3) | collective-permute-done | bytes 4194336 | tf_op jit(solution)/shard_map/ppermute | solution.py:199
  288.2 0.2 collective-permute-done.1.xb_hbm
  288.3 1.9 copy-done.3
  290.2 0.3 collective-permute-start.13
  290.5 1.2 collective-permute-start.12
  291.7 0.6 convert_reduce_fusion.2.cnt
  292.3 0.7 convert_reduce_fusion.1.cnt
  293.1 0.6 convert_reduce_fusion.cnt
  293.7 0.6 slice_bitcast_fusion.4
  294.3 0.6 slice_bitcast_fusion.3
  295.0 0.6 slice_bitcast_fusion.2
  295.6 108.2 %shard_map.102 = bf16[2048,2048]{1,0:T(8,128)(2,1)} custom-call(s32[16,384]{1,0:T(8,128)} %get-tuple-element.42.tok, f32[16,384]{1,0:T(8,128)} %get-tuple-element.41.gate, s32[16]{0:T(128)} %convert_reduce_fusion.1.cnt, bf16[1024,16,128]{2,1,0:T(8,128)(2,1)} %collective-permute-done.2.xa_hbm, bf16[1024,16,128]{2,1,0:T(8,128)(2,1)} %copy-done.3, ...), custom_call_target="tpu_custom_call" | custom-call | flops 55364812800 | bytes 276824064 | tf_op jit(solution)/shard_map/pallas_call | solution.py:167
  403.8 125.6 %shard_map.103 = bf16[2048,2048]{1,0:T(8,128)(2,1)} custom-call(s32[16,384]{1,0:T(8,128)} %get-tuple-element.46.tok, f32[16,384]{1,0:T(8,128)} %get-tuple-element.45.gate, s32[16]{0:T(128)} %convert_reduce_fusion.cnt, bf16[1024,16,128]{2,1,0:T(8,128)(2,1)} %collective-permute-done.12.xa_hbm, bf16[1024,16,128]{2,1,0:T(8,128)(2,1)} %collective-permute-done.13.xb_hbm, ...), custom_call_target="tpu_custom_call" | custom-call | flops 55364812800 | bytes 276824064 | tf_op jit(solution)/shard_map/pallas_call | solution.py:167
  529.5 9.4 %collective-permute-start.14 = (bf16[2048,2048]{1,0:T(8,128)(2,1)}, bf16[2048,2048]{1,0:T(8,128)(2,1)}, u32[]{:S(2)}, u32[]{:S(2)}) collective-permute-start(bf16[2048,2048]{1,0:T(8,128)(2,1)} %shard_map.103), channel_id=1, source_target_pairs={{0,6},{1,7},{2,4},{3,5},{4,2},{5,3},{6,0},{7,1}} | collective-permute-start | bytes 25165832 | tf_op jit(solution)/shard_map/ppermute | solution.py:199
  538.9 133.5 %shard_map.101 = bf16[2048,2048]{1,0:T(8,128)(2,1)} custom-call(s32[16,384]{1,0:T(8,128)} %get-tuple-element.38.tok, f32[16,384]{1,0:T(8,128)} %get-tuple-element.37.gate, s32[16]{0:T(128)} %convert_reduce_fusion.2.cnt, bf16[1024,16,128]{2,1,0:T(8,128)(2,1)} %collective-permute-done.xa_hbm, bf16[1024,16,128]{2,1,0:T(8,128)(2,1)} %collective-permute-done.1.xb_hbm, ...), custom_call_target="tpu_custom_call" | custom-call | flops 55364812800 | bytes 276824064 | tf_op jit(solution)/shard_map/pallas_call | solution.py:167
  672.4 3.0 collective-permute-start.11
  675.4 0.7 convert_reduce_fusion.3.cnt
  676.1 0.6 slice_bitcast_fusion.5
  676.7 120.2 %shard_map.100 = f32[2048,2048]{1,0:T(8,128)} custom-call(s32[16,384]{1,0:T(8,128)} %get-tuple-element.34.tok, f32[16,384]{1,0:T(8,128)} %get-tuple-element.33.gate, s32[16]{0:T(128)} %convert_reduce_fusion.3.cnt, bf16[1024,16,128]{2,1,0:T(8,128)(2,1)} %bitcast.11.xa_hbm, bf16[1024,16,128]{2,1,0:T(8,128)(2,1)} %bitcast.52, bf16[8,2048,1408]{2,1,0:T(8,128)(2,1)} %w1a.7, ...), custom_call_target="tpu_custom_call" | custom-call | flops 55364812800 | bytes 276824064 | tf_op jit(solution)/shard_map/pallas_call | solution.py:167
  796.9 93.4 %collective-permute-done.10 = bf16[2048,2048]{1,0:T(8,128)(2,1)} collective-permute-done((bf16[2048,2048]{1,0:T(8,128)(2,1)}, bf16[2048,2048]{1,0:T(8,128)(2,1)}, u32[]{:S(2)}, u32[]{:S(2)}) %collective-permute-start.10) | collective-permute-done | bytes 8388640 | tf_op jit(solution)/shard_map/ppermute | solution.py:199
  890.4 9.9 %collective-permute-done.11 = bf16[2048,2048]{1,0:T(8,128)(2,1)} collective-permute-done((bf16[2048,2048]{1,0:T(8,128)(2,1)}, bf16[2048,2048]{1,0:T(8,128)(2,1)}, u32[]{:S(2)}, u32[]{:S(2)}) %collective-permute-start.11) | collective-permute-done | bytes 8388640 | tf_op jit(solution)/shard_map/ppermute | solution.py:199
  900.3 23.5 %add_convert_fusion = bf16[2048,2048]{1,0:T(8,128)(2,1)} fusion(bf16[2048,2048]{1,0:T(8,128)(2,1)} %collective-permute-done.14, bf16[2048,2048]{1,0:T(8,128)(2,1)} %collective-permute-done.11, bf16[2048,2048]{1,0:T(8,128)(2,1)} %collective-permute-done.10, f32[2048,2048]{1,0:T(8,128)} %fusion.1, f32[2048,2048]{1,0:T(8,128)} %shard_map.100), kind=kLoop, calls=%fused_computation.4 | loop fusion | flops 33554432 | bytes 67108864 | tf_op jit(solution)/shard_map/convert_element_type | solution.py:250
  (47 shorter events, 0.2 us)
Async XLA Ops:
  0.0 3.9 copy-start
  0.0 295.6 %collective-permute-start.7 = (bf16[8,2048,1408]{2,1,0:T(8,128)(2,1)}, bf16[8,2048,1408]{2,1,0:T(8,128)(2,1)}, u32[]{:S(2)}, u32[]{:S(2)}) collective-permute-start(bf16[8,2048,1408]{2,1,0:T(8,128)(2,1)} %w1a.7), channel_id=1, source_target_pairs={{0,1},{1,0},{2,3},{3,2},{4,5},{5,4},{6,7},{7,6}} | collective-permute-start | bytes 138412032 | tf_op jit(solution)/shard_map/ppermute | solution.py:199
  0.0 295.6 %collective-permute-start.8 = (bf16[8,2048,1408]{2,1,0:T(8,128)(2,1)}, bf16[8,2048,1408]{2,1,0:T(8,128)(2,1)}, u32[]{:S(2)}, u32[]{:S(2)}) collective-permute-start(bf16[8,2048,1408]{2,1,0:T(8,128)(2,1)} %w3a.7), channel_id=1, source_target_pairs={{0,1},{1,0},{2,3},{3,2},{4,5},{5,4},{6,7},{7,6}} | collective-permute-start | bytes 138412032 | tf_op jit(solution)/shard_map/ppermute | solution.py:199
  0.5 295.1 %collective-permute-start.9 = (bf16[8,1408,2048]{2,1,0:T(8,128)(2,1)}, bf16[8,1408,2048]{2,1,0:T(8,128)(2,1)}, u32[]{:S(2)}, u32[]{:S(2)}) collective-permute-start(bf16[8,1408,2048]{2,1,0:T(8,128)(2,1)} %w2a.7), channel_id=1, source_target_pairs={{0,1},{1,0},{2,3},{3,2},{4,5},{5,4},{6,7},{7,6}} | collective-permute-start | bytes 138412032 | tf_op jit(solution)/shard_map/ppermute | solution.py:199
  53.1 34.2 %collective-permute-start.4 = (f32[16,2,384]{2,0,1:T(8,128)S(1)}, f32[16,2,384]{2,0,1:T(8,128)S(1)}, u32[]{:S(2)}, u32[]{:S(2)}) collective-permute-start(f32[16,2,384]{2,0,1:T(8,128)S(1)} %get-tuple-element.30), channel_id=1, source_target_pairs={{0,2},{1,3},{2,0},{3,1},{4,6},{5,7},{6,4},{7,5}} | collective-permute-start | bytes 147464 | tf_op jit(solution)/shard_map/ppermute | solution.py:199
  54.6 34.9 %slice-start = ((s8[8388608]{0:T(1024)(128)(4,1)}), s8[4194304]{0:T(1024)(128)(4,1)S(1)}, s32[]{:S(2)}) async-start(s8[8388608]{0:T(1024)(128)(4,1)} %bitcast.48), calls=%async_computation | async-start | bytes 8388608
  54.6 34.9 %slice-start.1 = ((s8[8388608]{0:T(1024)(128)(4,1)}), s8[4194304]{0:T(1024)(128)(4,1)S(1)}, s32[]{:S(2)}) async-start(s8[8388608]{0:T(1024)(128)(4,1)} %bitcast.48), calls=%async_computation.1 | async-start | bytes 8388608
  54.6 49.3 %collective-permute-start.5 = (f32[16,2,384]{2,0,1:T(8,128)S(1)}, f32[16,2,384]{2,0,1:T(8,128)S(1)}, u32[]{:S(2)}, u32[]{:S(2)}) collective-permute-start(f32[16,2,384]{2,0,1:T(8,128)S(1)} %get-tuple-element.31), channel_id=1, source_target_pairs={{0,4},{1,5},{2,6},{3,7},{4,0},{5,1},{6,2},{7,3}} | collective-permute-start | bytes 147464 | tf_op jit(solution)/shard_map/ppermute | solution.py:199
  87.3 0.6 copy-start.9
  87.9 16.4 %collective-permute-start.6 = (f32[16,2,384]{2,0,1:T(8,128)S(1)}, f32[16,2,384]{2,0,1:T(8,128)S(1)}, u32[]{:S(2)}, u32[]{:S(2)}) collective-permute-start(f32[16,2,384]{2,0,1:T(8,128)S(1)} %get-tuple-element.32), channel_id=1, source_target_pairs={{0,6},{1,7},{2,4},{3,5},{4,2},{5,3},{6,0},{7,1}} | collective-permute-start | bytes 147464 | tf_op jit(solution)/shard_map/ppermute | solution.py:199
  96.8 100.1 %copy-start.2 = (bf16[128,8,16,128]{3,2,1,0:T(8,128)(2,1)}, bf16[128,8,16,128]{3,2,1,0:T(8,128)(2,1)S(1)}, u32[]{:S(2)}) copy-start(bf16[128,8,16,128]{3,2,1,0:T(8,128)(2,1)S(1)} %copy.17) | copy-start | bytes 12582916
  103.9 36.5 %copy-start.5 = (f32[16,2,384]{2,0,1:T(8,128)}, f32[16,2,384]{2,0,1:T(8,128)S(1)}, u32[]{:S(2)}) copy-start(f32[16,2,384]{2,0,1:T(8,128)S(1)} %collective-permute-done.5) | copy-start | bytes 147460
  103.9 92.7 %collective-permute-start.2 = (bf16[1024,16,128]{2,1,0:T(8,128)(2,1)}, bf16[1024,16,128]{2,1,0:T(8,128)(2,1)}, u32[]{:S(2)}, u32[]{:S(2)}) collective-permute-start(bf16[1024,16,128]{2,1,0:T(8,128)(2,1)} %bitcast.11.xa_hbm), channel_id=1, source_target_pairs={{0,4},{1,5},{2,6},{3,7},{4,0},{5,1},{6,2},{7,3}} | collective-permute-start | bytes 12582920 | tf_op jit(solution)/shard_map/ppermute | solution.py:199
  104.3 36.1 %copy-start.7 = (f32[16,2,384]{2,0,1:T(8,128)}, f32[16,2,384]{2,0,1:T(8,128)S(1)}, u32[]{:S(2)}) copy-start(f32[16,2,384]{2,0,1:T(8,128)S(1)} %collective-permute-done.6) | copy-start | bytes 147460
  104.3 92.7 %collective-permute-start = (bf16[1024,16,128]{2,1,0:T(8,128)(2,1)}, bf16[1024,16,128]{2,1,0:T(8,128)(2,1)}, u32[]{:S(2)}, u32[]{:S(2)}) collective-permute-start(bf16[1024,16,128]{2,1,0:T(8,128)(2,1)} %bitcast.11.xa_hbm), channel_id=1, source_target_pairs={{0,2},{1,3},{2,0},{3,1},{4,6},{5,7},{6,4},{7,5}} | collective-permute-start | bytes 12582920 | tf_op jit(solution)/shard_map/ppermute | solution.py:199
  196.6 95.1 %copy-start.10 = (f32[16,2,384]{2,0,1:T(8,128)S(1)}, f32[16,2,384]{2,0,1:T(8,128)}, u32[]{:S(2)}) copy-start(f32[16,2,384]{2,0,1:T(8,128)} %copy-done.9) | copy-start | bytes 147460
  196.6 95.7 %copy-start.6 = (f32[16,2,384]{2,0,1:T(8,128)S(1)}, f32[16,2,384]{2,0,1:T(8,128)}, u32[]{:S(2)}) copy-start(f32[16,2,384]{2,0,1:T(8,128)} %copy-done.5) | copy-start | bytes 147460
  196.6 96.4 %copy-start.8 = (f32[16,2,384]{2,0,1:T(8,128)S(1)}, f32[16,2,384]{2,0,1:T(8,128)}, u32[]{:S(2)}) copy-start(f32[16,2,384]{2,0,1:T(8,128)} %copy-done.7) | copy-start | bytes 147460
  196.6 91.5 %collective-permute-start.3 = (bf16[1024,16,128]{2,1,0:T(8,128)(2,1)S(1)}, bf16[1024,16,128]{2,1,0:T(8,128)(2,1)S(1)}, u32[]{:S(2)}, u32[]{:S(2)}) collective-permute-start(bf16[1024,16,128]{2,1,0:T(8,128)(2,1)S(1)} %bitcast.50), channel_id=1, source_target_pairs={{0,4},{1,5},{2,6},{3,7},{4,0},{5,1},{6,2},{7,3}} | collective-permute-start | bytes 12582920 | tf_op jit(solution)/shard_map/ppermute | solution.py:199
  196.9 91.4 %collective-permute-start.1 = (bf16[1024,16,128]{2,1,0:T(8,128)(2,1)S(1)}, bf16[1024,16,128]{2,1,0:T(8,128)(2,1)}, u32[]{:S(2)}, u32[]{:S(2)}) collective-permute-start(bf16[1024,16,128]{2,1,0:T(8,128)(2,1)S(1)} %bitcast.51), channel_id=1, source_target_pairs={{0,2},{1,3},{2,0},{3,1},{4,6},{5,7},{6,4},{7,5}} | collective-permute-start | bytes 12582920 | tf_op jit(solution)/shard_map/ppermute | solution.py:199
  288.2 2.0 copy-start.3
  290.2 113.6 %collective-permute-start.13 = (bf16[1024,16,128]{2,1,0:T(8,128)(2,1)}, bf16[1024,16,128]{2,1,0:T(8,128)(2,1)}, u32[]{:S(2)}, u32[]{:S(2)}) collective-permute-start(bf16[1024,16,128]{2,1,0:T(8,128)(2,1)} %collective-permute-done.1.xb_hbm), channel_id=1, source_target_pairs={{0,4},{1,5},{2,6},{3,7},{4,0},{5,1},{6,2},{7,3}} | collective-permute-start | bytes 12582920 | tf_op jit(solution)/shard_map/ppermute | solution.py:199
  290.5 113.4 %collective-permute-start.12 = (bf16[1024,16,128]{2,1,0:T(8,128)(2,1)}, bf16[1024,16,128]{2,1,0:T(8,128)(2,1)}, u32[]{:S(2)}, u32[]{:S(2)}) collective-permute-start(bf16[1024,16,128]{2,1,0:T(8,128)(2,1)} %collective-permute-done.2.xa_hbm), channel_id=1, source_target_pairs={{0,2},{1,3},{2,0},{3,1},{4,6},{5,7},{6,4},{7,5}} | collective-permute-start | bytes 12582920 | tf_op jit(solution)/shard_map/ppermute | solution.py:199
  529.5 267.4 %collective-permute-start.14 = (bf16[2048,2048]{1,0:T(8,128)(2,1)}, bf16[2048,2048]{1,0:T(8,128)(2,1)}, u32[]{:S(2)}, u32[]{:S(2)}) collective-permute-start(bf16[2048,2048]{1,0:T(8,128)(2,1)} %shard_map.103), channel_id=1, source_target_pairs={{0,6},{1,7},{2,4},{3,5},{4,2},{5,3},{6,0},{7,1}} | collective-permute-start | bytes 25165832 | tf_op jit(solution)/shard_map/ppermute | solution.py:199
  538.9 136.5 %copy-start.4 = (f32[16,2,384]{2,0,1:T(8,128)S(1)}, f32[16,2,384]{2,0,1:T(8,128)}, u32[]{:S(2)}) copy-start(f32[16,2,384]{2,0,1:T(8,128)} %get-tuple-element.29) | copy-start | bytes 147460
  672.4 218.0 %collective-permute-start.10 = (bf16[2048,2048]{1,0:T(8,128)(2,1)}, bf16[2048,2048]{1,0:T(8,128)(2,1)}, u32[]{:S(2)}, u32[]{:S(2)}) collective-permute-start(bf16[2048,2048]{1,0:T(8,128)(2,1)} %shard_map.101), channel_id=1, source_target_pairs={{0,2},{1,3},{2,0},{3,1},{4,6},{5,7},{6,4},{7,5}} | collective-permute-start | bytes 25165832 | tf_op jit(solution)/shard_map/ppermute | solution.py:199
  672.4 227.9 %collective-permute-start.11 = (bf16[2048,2048]{1,0:T(8,128)(2,1)}, bf16[2048,2048]{1,0:T(8,128)(2,1)}, u32[]{:S(2)}, u32[]{:S(2)}) collective-permute-start(bf16[2048,2048]{1,0:T(8,128)(2,1)} %shard_map.102), channel_id=1, source_target_pairs={{0,4},{1,5},{2,6},{3,7},{4,0},{5,1},{6,2},{7,3}} | collective-permute-start | bytes 25165832 | tf_op jit(solution)/shard_map/ppermute | solution.py:199
  900.3 23.5 %copy-start.1 = (bf16[2048,64]{0,1:T(8,128)(2,1)S(1)}, bf16[2048,64]{0,1:T(8,128)(2,1)}, u32[]{:S(2)}) copy-start(bf16[2048,64]{0,1:T(8,128)(2,1)} %param.11) | copy-start | bytes 786436
where the time goes:
time: 935 us; the launch traced here: 924 us
  Pallas kernels  488 us (52%)
  waiting for transfers between devices  218 us (23%)
  matrix products  106 us (11%)
  other arithmetic  72.7 us (8%)
  starting transfers between devices  21.6 us (2%)
  local copies, waits for them, and re-layouts  17.5 us (2%)
    pallas_call x4, Pallas kernels, expert_bank(): pl.pallas_call(bank_kernel, out_shape=jax.ShapeDtypeStruct((tokens, width...  488 us
    ppermute x15, waiting for transfers between devices, swap(): return lax.ppermute(a, 'ep', [(i, i ^ s) for i in range(groups)])  218 us
    reduce_sum x1, other arithmetic, device_fn(): slot_gate = jnp.sum(jnp.where(hit, prob[:, :, None], 0.0), axis=0)  41.9 us
    dot_general x1, matrix products, swiglu(): h_up = jnp.dot(tok_rows, up_w, preferred_element_type=jnp.float32)  34.6 us
    dot_general x1, matrix products, swiglu(): h_gate = jnp.dot(tok_rows, gate_w, preferred_element_type=jnp.float32)  32.2 us
    dot_general x1, matrix products, swiglu(): return jnp.dot(act_rows, down_w, preferred_element_type=jnp.float32)  31.8 us
    convert_element_type x1, other arithmetic, device_fn(): return total.astype(jnp.bfloat16)  23.5 us
    ppermute x15, starting transfers between devices, swap(): return lax.ppermute(a, 'ep', [(i, i ^ s) for i in range(groups)])  21.6 us
  transfers between devices with their start and end apart: 15, of which 5 were waited for; matrix products, arithmetic and copies ran while one was open for 18% of the time, Pallas kernels for 39%

commit v1 on v0

--- a/solution.py
+++ b/solution.py
@@ -8,7 +8,7 @@
 ROUTE_SCALE = 16.0
 CAP = 384
 LANES = 128
-STRIDE = CAP + 8
+STRIDE = CAP + 4
 SIZES = (64, 128, 192, 256, 320, 384)
 UNROLL = 16
 BATCH = 8
@@ -23,7 +23,8 @@
 
 def bank_kernel(tok, gate, cnt, xa_hbm, xb_hbm, w1a, w3a, w2a, w1b, w3b, w2b, out_hbm,
                 x_v, acc, w1v, w3v, w2v, xf, xs, hv, stage, x_sem, w1_sem, w3_sem, w2_sem, out_sem):
-    tokens, chunks, _ = x_v.shape
+    _, chunks, _ = x_v.shape
+    tokens = out_hbm.shape[0]
     width = chunks * LANES
     per_dev = w1a.shape[0]
     ff = w1a.shape[2]
@@ -81,7 +82,7 @@
         def _(c):
             o = jnp.dot(hv[0:m, :], w2v[:, pl.ds(pl.multiple_of(c * cols, cols), cols)], preferred_element_type=jnp.float32)
             o = o.astype(jnp.bfloat16).astype(jnp.float32)
-            base = pl.multiple_of(c * (cols // LANES * STRIDE), 8)
+            base = c * (cols // LANES * STRIDE)
             for j in range(cols // LANES):
                 xf[pl.ds(base + j * STRIDE, m), :] = o[:, j * LANES:(j + 1) * LANES]
 
@@ -89,6 +90,7 @@
     def _(e):
         slot = lax.rem(e, 2)
         n = cnt[e]
+        first_pair = e * CAP
 
         @pl.when(e + 1 < experts)
         def _():
@@ -98,8 +100,7 @@
         def _(g):
             s0 = pl.multiple_of(g * UNROLL, UNROLL)
             for i in range(UNROLL):
-                t = jnp.minimum(tok[e, s0 + i], tokens - 1)
-                xf[pl.ds(s0 + i, chunks, stride=STRIDE), :] = x_v[t].astype(jnp.float32)
+                xf[pl.ds(s0 + i, chunks, stride=STRIDE), :] = x_v[tok[first_pair + s0 + i]].astype(jnp.float32)
 
         in_copies(e, slot, False)
         lo = 0
@@ -126,12 +127,12 @@
         @pl.loop(0, (n + UNROLL - 1) // UNROLL)
         def _(g):
             s0 = pl.multiple_of(g * UNROLL, UNROLL)
-            for first in range(0, UNROLL, BATCH):
+            for b in range(0, UNROLL, BATCH):
                 sums = []
-                for i in range(first, first + BATCH):
-                    base = pl.multiple_of(tok[e, s0 + i] * chunks, chunks)
+                for i in range(b, b + BATCH):
+                    base = pl.multiple_of(tok[first_pair + s0 + i] * chunks, chunks)
                     row = xf[pl.ds(s0 + i, chunks, stride=STRIDE), :]
-                    sums.append((base, acc[pl.ds(base, chunks), :] + gate[e, s0 + i] * row))
+                    sums.append((base, acc[pl.ds(base, chunks), :] + gate[first_pair + s0 + i] * row))
                 for base, val in sums:
                     acc[pl.ds(base, chunks), :] = val
 
@@ -170,7 +171,7 @@
         in_specs=[smem] * 3 + [anys] * 8,
         out_specs=anys,
         scratch_shapes=[
-            pltpu.VMEM((tokens, chunks, LANES), jnp.bfloat16),
+            pltpu.VMEM((tokens + 8, chunks, LANES), jnp.bfloat16),
             pltpu.VMEM(((tokens + 16) * chunks, LANES), jnp.float32),
             pltpu.VMEM((2, width, ff), jnp.bfloat16),
             pltpu.VMEM((2, width, ff), jnp.bfloat16),
@@ -187,7 +188,7 @@
         ],
         compiler_params=pltpu.CompilerParams(vmem_limit_bytes=66_000_000),
         cost_estimate=pl.CostEstimate(flops=flops, bytes_accessed=6 * per_dev * width * ff * 2, transcendentals=0),
-    )(tok, gate, cnt, *x3, *w_own, *w_peer)
+    )(tok.reshape(-1), gate.reshape(-1), cnt, *x3, *w_own, *w_peer)
 
 
 def solution(mesh):
@@ -245,8 +246,10 @@
         x6, part4 = lax.optimization_barrier((x6, part4))
         back6 = swap(run(x6, l_in[6], jnp.bfloat16), 6)
         total = shared + run(x0, lists_of(me), jnp.float32)
-        for b in (back2, back4, back6):
+        for b in (back2, back4):
             total = total + b.astype(jnp.float32)
+        total, back6 = lax.optimization_barrier((total, back6))
+        total = total + back6.astype(jnp.float32)
         return total.astype(jnp.bfloat16)
 
     return jax.shard_map(device_fn, mesh=mesh, in_specs=(tok_spec, P(), bank_spec, bank_spec, bank_spec, P(), P(), P(), tok_spec, tok_spec), out_specs=tok_spec, check_vma=False)

time: 935 us -> 899 us (0.961)
  Pallas kernels: 488 us -> 441 us
    pallas_call x4, Pallas kernels: 488 us -> 441 us  [expert_bank(): pl.pallas_call(bank_kernel, out_shape=jax.ShapeDtypeStruct((tokens, width...]
    add x0 -> x1, other arithmetic: none -> 17 us  [device_fn(): total = total + b.astype(jnp.float32)]
    convert_element_type x1, other arithmetic: 23.5 us -> 8.42 us  [device_fn(): return total.astype(jnp.bfloat16)]
  transfers between devices with their start and end apart: 15 -> 15, of which waited for: 5 -> 3; matrix products, arithmetic and copies ran while one was open for 18% -> 21% of each run, Pallas kernels for 39% -> 50%
where the time goes in v1:
time: 899 us; the launch traced here: 889 us
  Pallas kernels  441 us (49%)
  waiting for transfers between devices  227 us (25%)
  matrix products  106 us (12%)
  other arithmetic  72.3 us (8%)
  local copies, waits for them, and re-layouts  23.8 us (3%)
  starting transfers between devices  19 us (2%)
    pallas_call x4, Pallas kernels, expert_bank(): pl.pallas_call(bank_kernel, out_shape=jax.ShapeDtypeStruct((tokens, width...  441 us
    ppermute x15, waiting for transfers between devices, swap(): return lax.ppermute(a, 'ep', [(i, i ^ s) for i in range(groups)])  227 us
    reduce_sum x1, other arithmetic, device_fn(): slot_gate = jnp.sum(jnp.where(hit, prob[:, :, None], 0.0), axis=0)  41.9 us
    dot_general x1, matrix products, swiglu(): h_up = jnp.dot(tok_rows, up_w, preferred_element_type=jnp.float32)  34.7 us
    dot_general x1, matrix products, swiglu(): h_gate = jnp.dot(tok_rows, gate_w, preferred_element_type=jnp.float32)  32.2 us
    dot_general x1, matrix products, swiglu(): return jnp.dot(act_rows, down_w, preferred_element_type=jnp.float32)  31.9 us
    ppermute x15, starting transfers between devices, swap(): return lax.ppermute(a, 'ep', [(i, i ^ s) for i in range(groups)])  19 us
    unnamed x31, local copies, waits for them, and re-layouts  18.3 us
  transfers between devices with their start and end apart: 15, of which 3 were waited for; matrix products, arithmetic and copies ran while one was open for 21% of the time, Pallas kernels for 50%

profile of v1, /device:TPU:4, one launch (start us, length us, event | category | flops | bytes accessed | tf_op | source)
XLA Modules:
  0.0 889.1 jit_solution(9157622014847522634)
XLA Ops:
  0.0 0.5 collective-permute-start.8
  0.5 0.9 compare_select_fusion
  1.4 0.5 fusion.2
  1.9 1.7 fusion.4
  3.6 0.3 copy.14
  3.9 6.0 fusion.19
  10.6 41.9 %select_reduce_fusion = (f32[64,384]{1,0:T(8,128)S(1)}, f32[64,384]{1,0:T(8,128)S(1)}) fusion(f32[2048,64]{1,0:T(8,128)S(1)} %copy.15, s32[2048,64]{1,0:T(8,128)S(1)} %copy.14, f32[2048]{0:T(1024)S(1)} %iota_convert_fusion), kind=kLoop, calls=%fused_computation | loop fusion | flops 251609088 | bytes 1253376 | tf_op jit(solution)/shard_map/reduce_sum | solution.py:225
  52.5 0.6 fusion.6
  53.1 1.5 collective-permute-start.4
  54.6 0.5 collective-permute-start.5
  55.1 32.2 %fusion.20 = f32[2048,2816]{1,0:T(8,128)} fusion(bf16[2048,2048]{1,0:T(8,128)(2,1)} %param.10, bf16[2048,2816]{1,0:T(8,128)(2,1)} %param.15), kind=kOutput, calls=%fused_computation.54 | convolution fusion | flops 23622320128 | bytes 42991616 | tf_op jit(solution)/shard_map/dot_general | solution.py:18
  87.3 0.6 copy-done.10
  87.9 1.6 collective-permute-start.6
  89.5 3.7 slice_bitcast_fusion
  93.2 3.6 copy.17
  96.8 7.1 copy.16
  103.9 0.4 collective-permute-start.2
  104.3 1.5 collective-permute-start
  105.8 34.7 %multiply_convert_fusion.clone.4 = bf16[2048,2816]{1,0:T(8,128)(2,1)} fusion(f32[2048,2816]{1,0:T(8,128)} %fusion.20, bf16[2048,2048]{1,0:T(8,128)(2,1)} %param.10, bf16[2048,2816]{1,0:T(8,128)(2,1)} %param.16), kind=kOutput, calls=%fused_computation.3.clone.clone.clone.1 | convolution fusion | flops 23656923136 | bytes 54525952 | tf_op jit(solution)/shard_map/dot_general | solution.py:19
  140.5 56.2 %collective-permute-done.2.xa_hbm = bf16[1024,16,128]{2,1,0:T(8,128)(2,1)} collective-permute-done((bf16[1024,16,128]{2,1,0:T(8,128)(2,1)}, bf16[1024,16,128]{2,1,0:T(8,128)(2,1)}, u32[]{:S(2)}, u32[]{:S(2)}) %collective-permute-start.2) | collective-permute-done | bytes 4194336 | tf_op jit(solution)/shard_map/ppermute | solution.py:200
  196.9 1.4 collective-permute-start.1
  198.3 31.9 %fusion.1 = f32[2048,2048]{1,0:T(8,128)} fusion(bf16[2816,2048]{1,0:T(8,128)(2,1)} %param.17, bf16[2048,2816]{1,0:T(8,128)(2,1)} %multiply_convert_fusion.clone.4), kind=kOutput, calls=%fused_computation.8 | convolution fusion | flops 23622320128 | bytes 39845888 | tf_op jit(solution)/shard_map/dot_general | solution.py:21
  230.2 58.0 %collective-permute-done.3.xb_hbm = bf16[1024,16,128]{2,1,0:T(8,128)(2,1)S(1)} collective-permute-done((bf16[1024,16,128]{2,1,0:T(8,128)(2,1)S(1)}, bf16[1024,16,128]{2,1,0:T(8,128)(2,1)S(1)}, u32[]{:S(2)}, u32[]{:S(2)}) %collective-permute-start.3) | collective-permute-done | bytes 4194336 | tf_op jit(solution)/shard_map/ppermute | solution.py:200
  288.3 2.0 copy-done.3
  290.3 1.2 copy-done.4
  291.5 0.6 reshape_squeeze.13.gate
  292.1 0.6 convert_element_type.83.tok
  292.8 0.6 reshape_squeeze.14.gate
  293.4 0.6 convert_element_type.87.tok
  294.0 0.6 reshape_squeeze.15.gate
  294.6 0.6 convert_element_type.91.tok
  295.2 0.4 collective-permute-start.13
  295.7 1.1 collective-permute-start.12
  296.7 0.7 convert_reduce_fusion.2.cnt
  297.4 0.7 convert_reduce_fusion.1.cnt
  298.1 0.6 convert_reduce_fusion.cnt
  298.7 97.4 %shard_map.102 = bf16[2048,2048]{1,0:T(8,128)(2,1)} custom-call(s32[6144]{0:T(1024)} %convert_element_type.87.tok, f32[6144]{0:T(1024)} %reshape_squeeze.14.gate, s32[16]{0:T(128)} %convert_reduce_fusion.1.cnt, bf16[1024,16,128]{2,1,0:T(8,128)(2,1)} %collective-permute-done.2.xa_hbm, bf16[1024,16,128]{2,1,0:T(8,128)(2,1)} %copy-done.4, ...), custom_call_target="tpu_custom_call" | custom-call | flops 55364812800 | bytes 276824064 | tf_op jit(solution)/shard_map/pallas_call | solution.py:168
  396.1 2.2 collective-permute-start.11
  398.4 121.6 %shard_map.101 = bf16[2048,2048]{1,0:T(8,128)(2,1)} custom-call(s32[6144]{0:T(1024)} %convert_element_type.83.tok, f32[6144]{0:T(1024)} %reshape_squeeze.13.gate, s32[16]{0:T(128)} %convert_reduce_fusion.2.cnt, bf16[1024,16,128]{2,1,0:T(8,128)(2,1)} %collective-permute-done.xa_hbm, bf16[1024,16,128]{2,1,0:T(8,128)(2,1)} %copy-done.3, ...), custom_call_target="tpu_custom_call" | custom-call | flops 55364812800 | bytes 276824064 | tf_op jit(solution)/shard_map/pallas_call | solution.py:168
  520.0 114.0 %shard_map.103 = bf16[2048,2048]{1,0:T(8,128)(2,1)} custom-call(s32[6144]{0:T(1024)} %convert_element_type.91.tok, f32[6144]{0:T(1024)} %reshape_squeeze.15.gate, s32[16]{0:T(128)} %convert_reduce_fusion.cnt, bf16[1024,16,128]{2,1,0:T(8,128)(2,1)} %collective-permute-done.12.xa_hbm, bf16[1024,16,128]{2,1,0:T(8,128)(2,1)} %collective-permute-done.13.xb_hbm, ...), custom_call_target="tpu_custom_call" | custom-call | flops 55364812800 | bytes 276824064 | tf_op jit(solution)/shard_map/pallas_call | solution.py:168
  634.1 7.5 collective-permute-start.14
  641.7 0.6 reshape_squeeze.12.gate
  642.3 0.6 convert_element_type.80.tok
  642.9 0.7 convert_reduce_fusion.3.cnt
  643.6 107.5 %shard_map.100 = f32[2048,2048]{1,0:T(8,128)} custom-call(s32[6144]{0:T(1024)} %convert_element_type.80.tok, f32[6144]{0:T(1024)} %reshape_squeeze.12.gate, s32[16]{0:T(128)} %convert_reduce_fusion.3.cnt, bf16[1024,16,128]{2,1,0:T(8,128)(2,1)} %bitcast.3.xa_hbm, bf16[1024,16,128]{2,1,0:T(8,128)(2,1)} %bitcast.44, bf16[8,2048,1408]{2,1,0:T(8,128)(2,1)} %w1a.7, ...), custom_call_target="tpu_custom_call" | custom-call | flops 55364812800 | bytes 276824064 | tf_op jit(solution)/shard_map/pallas_call | solution.py:168
  751.1 17.0 %convert_add_fusion = f32[2048,2048]{1,0:T(8,128)S(1)} fusion(bf16[2048,2048]{1,0:T(8,128)(2,1)} %collective-permute-done.11, bf16[2048,2048]{1,0:T(8,128)(2,1)} %collective-permute-done.10, f32[2048,2048]{1,0:T(8,128)} %fusion.1, f32[2048,2048]{1,0:T(8,128)} %shard_map.100), kind=kLoop, calls=%fused_computation.5 | loop fusion | flops 20971520 | bytes 67108864 | tf_op jit(solution)/shard_map/add | solution.py:250
  768.1 112.4 %collective-permute-done.14 = bf16[2048,2048]{1,0:T(8,128)(2,1)} collective-permute-done((bf16[2048,2048]{1,0:T(8,128)(2,1)}, bf16[2048,2048]{1,0:T(8,128)(2,1)}, u32[]{:S(2)}, u32[]{:S(2)}) %collective-permute-start.14) | collective-permute-done | bytes 8388640 | tf_op jit(solution)/shard_map/ppermute | solution.py:200
  880.5 8.4 add_convert_fusion
  (58 shorter events, 1.1 us)
Async XLA Ops:
  0.0 3.9 copy-start
  0.0 298.7 %collective-permute-start.7 = (bf16[8,2048,1408]{2,1,0:T(8,128)(2,1)}, bf16[8,2048,1408]{2,1,0:T(8,128)(2,1)}, u32[]{:S(2)}, u32[]{:S(2)}) collective-permute-start(bf16[8,2048,1408]{2,1,0:T(8,128)(2,1)} %w1a.7), channel_id=1, source_target_pairs={{0,1},{1,0},{2,3},{3,2},{4,5},{5,4},{6,7},{7,6}} | collective-permute-start | bytes 138412032 | tf_op jit(solution)/shard_map/ppermute | solution.py:200
  0.0 298.7 %collective-permute-start.8 = (bf16[8,2048,1408]{2,1,0:T(8,128)(2,1)}, bf16[8,2048,1408]{2,1,0:T(8,128)(2,1)}, u32[]{:S(2)}, u32[]{:S(2)}) collective-permute-start(bf16[8,2048,1408]{2,1,0:T(8,128)(2,1)} %w3a.7), channel_id=1, source_target_pairs={{0,1},{1,0},{2,3},{3,2},{4,5},{5,4},{6,7},{7,6}} | collective-permute-start | bytes 138412032 | tf_op jit(solution)/shard_map/ppermute | solution.py:200
  0.5 298.2 %collective-permute-start.9 = (bf16[8,1408,2048]{2,1,0:T(8,128)(2,1)}, bf16[8,1408,2048]{2,1,0:T(8,128)(2,1)}, u32[]{:S(2)}, u32[]{:S(2)}) collective-permute-start(bf16[8,1408,2048]{2,1,0:T(8,128)(2,1)} %w2a.7), channel_id=1, source_target_pairs={{0,1},{1,0},{2,3},{3,2},{4,5},{5,4},{6,7},{7,6}} | collective-permute-start | bytes 138412032 | tf_op jit(solution)/shard_map/ppermute | solution.py:200
  53.1 34.2 %collective-permute-start.4 = (f32[16,2,384]{2,0,1:T(8,128)S(1)}, f32[16,2,384]{2,0,1:T(8,128)S(1)}, u32[]{:S(2)}, u32[]{:S(2)}) collective-permute-start(f32[16,2,384]{2,0,1:T(8,128)S(1)} %get-tuple-element.34), channel_id=1, source_target_pairs={{0,2},{1,3},{2,0},{3,1},{4,6},{5,7},{6,4},{7,5}} | collective-permute-start | bytes 147464 | tf_op jit(solution)/shard_map/ppermute | solution.py:200
  54.6 34.9 %slice-start = ((s8[8388608]{0:T(1024)(128)(4,1)}), s8[4194304]{0:T(1024)(128)(4,1)S(1)}, s32[]{:S(2)}) async-start(s8[8388608]{0:T(1024)(128)(4,1)} %bitcast.40), calls=%async_computation | async-start | bytes 8388608
  54.6 34.9 %slice-start.1 = ((s8[8388608]{0:T(1024)(128)(4,1)}), s8[4194304]{0:T(1024)(128)(4,1)S(1)}, s32[]{:S(2)}) async-start(s8[8388608]{0:T(1024)(128)(4,1)} %bitcast.40), calls=%async_computation.1 | async-start | bytes 8388608
  54.6 49.3 %collective-permute-start.5 = (f32[16,2,384]{2,0,1:T(8,128)S(1)}, f32[16,2,384]{2,0,1:T(8,128)S(1)}, u32[]{:S(2)}, u32[]{:S(2)}) collective-permute-start(f32[16,2,384]{2,0,1:T(8,128)S(1)} %get-tuple-element.35), channel_id=1, source_target_pairs={{0,4},{1,5},{2,6},{3,7},{4,0},{5,1},{6,2},{7,3}} | collective-permute-start | bytes 147464 | tf_op jit(solution)/shard_map/ppermute | solution.py:200
  87.3 0.6 copy-start.10
  87.9 16.4 %collective-permute-start.6 = (f32[16,2,384]{2,0,1:T(8,128)S(1)}, f32[16,2,384]{2,0,1:T(8,128)S(1)}, u32[]{:S(2)}, u32[]{:S(2)}) collective-permute-start(f32[16,2,384]{2,0,1:T(8,128)S(1)} %get-tuple-element.36), channel_id=1, source_target_pairs={{0,6},{1,7},{2,4},{3,5},{4,2},{5,3},{6,0},{7,1}} | collective-permute-start | bytes 147464 | tf_op jit(solution)/shard_map/ppermute | solution.py:200
  96.8 100.1 %copy-start.2 = (bf16[128,8,16,128]{3,2,1,0:T(8,128)(2,1)}, bf16[128,8,16,128]{3,2,1,0:T(8,128)(2,1)S(1)}, u32[]{:S(2)}) copy-start(bf16[128,8,16,128]{3,2,1,0:T(8,128)(2,1)S(1)} %copy.17) | copy-start | bytes 12582916
  103.9 36.5 %copy-start.8 = (f32[16,2,384]{2,0,1:T(8,128)}, f32[16,2,384]{2,0,1:T(8,128)S(1)}, u32[]{:S(2)}) copy-start(f32[16,2,384]{2,0,1:T(8,128)S(1)} %collective-permute-done.5) | copy-start | bytes 147460
  103.9 92.7 %collective-permute-start.2 = (bf16[1024,16,128]{2,1,0:T(8,128)(2,1)}, bf16[1024,16,128]{2,1,0:T(8,128)(2,1)}, u32[]{:S(2)}, u32[]{:S(2)}) collective-permute-start(bf16[1024,16,128]{2,1,0:T(8,128)(2,1)} %bitcast.3.xa_hbm), channel_id=1, source_target_pairs={{0,4},{1,5},{2,6},{3,7},{4,0},{5,1},{6,2},{7,3}} | collective-permute-start | bytes 12582920 | tf_op jit(solution)/shard_map/ppermute | solution.py:200
  104.3 36.2 %copy-start.6 = (f32[16,2,384]{2,0,1:T(8,128)}, f32[16,2,384]{2,0,1:T(8,128)S(1)}, u32[]{:S(2)}) copy-start(f32[16,2,384]{2,0,1:T(8,128)S(1)} %collective-permute-done.6) | copy-start | bytes 147460
  104.3 92.6 %collective-permute-start = (bf16[1024,16,128]{2,1,0:T(8,128)(2,1)}, bf16[1024,16,128]{2,1,0:T(8,128)(2,1)}, u32[]{:S(2)}, u32[]{:S(2)}) collective-permute-start(bf16[1024,16,128]{2,1,0:T(8,128)(2,1)} %bitcast.3.xa_hbm), channel_id=1, source_target_pairs={{0,2},{1,3},{2,0},{3,1},{4,6},{5,7},{6,4},{7,5}} | collective-permute-start | bytes 12582920 | tf_op jit(solution)/shard_map/ppermute | solution.py:200
  196.6 93.6 %copy-start.11 = (f32[16,2,384]{2,0,1:T(8,128)S(1)}, f32[16,2,384]{2,0,1:T(8,128)}, u32[]{:S(2)}) copy-start(f32[16,2,384]{2,0,1:T(8,128)} %copy-done.10) | copy-start | bytes 147460
  196.6 96.1 %copy-start.9 = (f32[16,2,384]{2,0,1:T(8,128)S(1)}, f32[16,2,384]{2,0,1:T(8,128)}, u32[]{:S(2)}) copy-start(f32[16,2,384]{2,0,1:T(8,128)} %copy-done.8) | copy-start | bytes 147460
  196.7 97.3 %copy-start.7 = (f32[16,2,384]{2,0,1:T(8,128)S(1)}, f32[16,2,384]{2,0,1:T(8,128)}, u32[]{:S(2)}) copy-start(f32[16,2,384]{2,0,1:T(8,128)} %copy-done.6) | copy-start | bytes 147460
  196.7 91.6 %collective-permute-start.3 = (bf16[1024,16,128]{2,1,0:T(8,128)(2,1)S(1)}, bf16[1024,16,128]{2,1,0:T(8,128)(2,1)S(1)}, u32[]{:S(2)}, u32[]{:S(2)}) collective-permute-start(bf16[1024,16,128]{2,1,0:T(8,128)(2,1)S(1)} %bitcast.42), channel_id=1, source_target_pairs={{0,4},{1,5},{2,6},{3,7},{4,0},{5,1},{6,2},{7,3}} | collective-permute-start | bytes 12582920 | tf_op jit(solution)/shard_map/ppermute | solution.py:200
  196.9 91.3 %collective-permute-start.1 = (bf16[1024,16,128]{2,1,0:T(8,128)(2,1)S(1)}, bf16[1024,16,128]{2,1,0:T(8,128)(2,1)S(1)}, u32[]{:S(2)}, u32[]{:S(2)}) collective-permute-start(bf16[1024,16,128]{2,1,0:T(8,128)(2,1)S(1)} %bitcast.43), channel_id=1, source_target_pairs={{0,2},{1,3},{2,0},{3,1},{4,6},{5,7},{6,4},{7,5}} | collective-permute-start | bytes 12582920 | tf_op jit(solution)/shard_map/ppermute | solution.py:200
  288.2 3.3 copy-start.4
  288.3 2.0 copy-start.3
  295.2 103.2 %collective-permute-start.13 = (bf16[1024,16,128]{2,1,0:T(8,128)(2,1)}, bf16[1024,16,128]{2,1,0:T(8,128)(2,1)}, u32[]{:S(2)}, u32[]{:S(2)}) collective-permute-start(bf16[1024,16,128]{2,1,0:T(8,128)(2,1)} %copy-done.3), channel_id=1, source_target_pairs={{0,4},{1,5},{2,6},{3,7},{4,0},{5,1},{6,2},{7,3}} | collective-permute-start | bytes 12582920 | tf_op jit(solution)/shard_map/ppermute | solution.py:200
  295.7 102.7 %collective-permute-start.12 = (bf16[1024,16,128]{2,1,0:T(8,128)(2,1)}, bf16[1024,16,128]{2,1,0:T(8,128)(2,1)}, u32[]{:S(2)}, u32[]{:S(2)}) collective-permute-start(bf16[1024,16,128]{2,1,0:T(8,128)(2,1)} %collective-permute-done.2.xa_hbm), channel_id=1, source_target_pairs={{0,2},{1,3},{2,0},{3,1},{4,6},{5,7},{6,4},{7,5}} | collective-permute-start | bytes 12582920 | tf_op jit(solution)/shard_map/ppermute | solution.py:200
  396.1 354.9 %collective-permute-start.11 = (bf16[2048,2048]{1,0:T(8,128)(2,1)}, bf16[2048,2048]{1,0:T(8,128)(2,1)}, u32[]{:S(2)}, u32[]{:S(2)}) collective-permute-start(bf16[2048,2048]{1,0:T(8,128)(2,1)} %shard_map.102), channel_id=1, source_target_pairs={{0,4},{1,5},{2,6},{3,7},{4,0},{5,1},{6,2},{7,3}} | collective-permute-start | bytes 25165832 | tf_op jit(solution)/shard_map/ppermute | solution.py:200
  520.0 121.6 %copy-start.5 = (f32[16,2,384]{2,0,1:T(8,128)S(1)}, f32[16,2,384]{2,0,1:T(8,128)}, u32[]{:S(2)}) copy-start(f32[16,2,384]{2,0,1:T(8,128)} %get-tuple-element.33) | copy-start | bytes 147460
  520.0 231.0 %collective-permute-start.10 = (bf16[2048,2048]{1,0:T(8,128)(2,1)}, bf16[2048,2048]{1,0:T(8,128)(2,1)}, u32[]{:S(2)}, u32[]{:S(2)}) collective-permute-start(bf16[2048,2048]{1,0:T(8,128)(2,1)} %shard_map.101), channel_id=1, source_target_pairs={{0,2},{1,3},{2,0},{3,1},{4,6},{5,7},{6,4},{7,5}} | collective-permute-start | bytes 25165832 | tf_op jit(solution)/shard_map/ppermute | solution.py:200
  634.1 246.4 %collective-permute-start.14 = (bf16[2048,2048]{1,0:T(8,128)(2,1)}, bf16[2048,2048]{1,0:T(8,128)(2,1)}, u32[]{:S(2)}, u32[]{:S(2)}) collective-permute-start(bf16[2048,2048]{1,0:T(8,128)(2,1)} %shard_map.103), channel_id=1, source_target_pairs={{0,6},{1,7},{2,4},{3,5},{4,2},{5,3},{6,0},{7,1}} | collective-permute-start | bytes 25165832 | tf_op jit(solution)/shard_map/ppermute | solution.py:200
  751.1 137.8 %copy-start.1 = (bf16[2048,64]{0,1:T(8,128)(2,1)S(1)}, bf16[2048,64]{0,1:T(8,128)(2,1)}, u32[]{:S(2)}) copy-start(bf16[2048,64]{0,1:T(8,128)(2,1)} %param.11) | copy-start | bytes 786436

commit v2 on v1

v2 whole, which is shorter than its diff:
```python
import jax
import jax.numpy as jnp
from jax import lax
from jax.experimental import pallas as pl
from jax.experimental.pallas import tpu as pltpu
from jax.sharding import PartitionSpec as P

ROUTE_SCALE = 16.0
CAP = 384
LANES = 128
STRIDE = CAP + 20
SIZES = (64, 128, 192, 256, 320, 384)
UNROLL = 16
BATCH = 8


def swiglu(tok_rows, gate_w, up_w, down_w):
    h_gate = jnp.dot(tok_rows, gate_w, preferred_element_type=jnp.float32)
    h_up = jnp.dot(tok_rows, up_w, preferred_element_type=jnp.float32)
    act_rows = (jax.nn.silu(h_gate) * h_up).astype(jnp.bfloat16)
    return jnp.dot(act_rows, down_w, preferred_element_type=jnp.float32)


def bank_kernel(tok, gate, cnt, xa_hbm, xb_hbm, w1a, w3a, w2a, w1b, w3b, w2b, outa_hbm, outb_hbm,
                x_v, acc, w1v, w3v, w2v, xf, xs, hv, stage, x_sem, w1_sem, w3_sem, w2_sem, out_sem):
    _, chunks, _ = x_v.shape
    tokens = 2 * outa_hbm.shape[0]
    width = chunks * LANES
    per_dev = w1a.shape[0]
    ff = w1a.shape[2]
    experts = 2 * per_dev

    def copy_w(dst, sem, a, b, e, start):
        @pl.when((e < per_dev) & (cnt[2 * e] + cnt[2 * e + 1] > 0))
        def _():
            c = pltpu.make_async_copy(a.at[jnp.minimum(e, per_dev - 1)], dst, sem)
            c.start() if start else c.wait()

        @pl.when((e >= per_dev) & (cnt[2 * e] + cnt[2 * e + 1] > 0))
        def _():
            c = pltpu.make_async_copy(b.at[jnp.maximum(e - per_dev, 0)], dst, sem)
            c.start() if start else c.wait()

    def in_copies(e, slot, start):
        copy_w(w1v.at[slot], w1_sem.at[slot], w1a, w1b, e, start)
        copy_w(w3v.at[slot], w3_sem.at[slot], w3a, w3b, e, start)

    half = tokens // 2
    x_copies = [pltpu.make_async_copy(src, x_v.at[pl.ds(i * half, half)], x_sem.at[i]) for i, src in enumerate((xa_hbm, xb_hbm))]
    for c in x_copies:
        c.start()
    in_copies(jnp.int32(0), 0, True)
    copy_w(w2v, w2_sem, w2a, w2b, jnp.int32(0), True)

    rows0 = acc.shape[0]
    zblk = 256

    @pl.loop(0, rows0 // zblk)
    def _(i):
        acc[pl.ds(pl.multiple_of(i * zblk, zblk), zblk), :] = jnp.zeros((zblk, LANES), jnp.float32)

    for c in x_copies:
        c.wait()

    def ffn(m, slot):
        for j in range(chunks):
            xs[0:m, j * LANES:(j + 1) * LANES] = xf[j * STRIDE:j * STRIDE + m, :].astype(jnp.bfloat16)

        def gate_up(c0, cw):
            xv = xs[0:m, :]
            g = jnp.dot(xv, w1v[slot, :, c0:c0 + cw], preferred_element_type=jnp.float32)
            u = jnp.dot(xv, w3v[slot, :, c0:c0 + cw], preferred_element_type=jnp.float32)
            hv[0:m, c0:c0 + cw] = (jax.nn.silu(g) * u).astype(jnp.bfloat16)

        for c0 in range(0, ff, 768):
            gate_up(c0, min(768, ff - c0))

    def down(m):
        cols = 1024

        @pl.loop(0, width // cols)
        def _(c):
            o = jnp.dot(hv[0:m, :], w2v[:, pl.ds(pl.multiple_of(c * cols, cols), cols)], preferred_element_type=jnp.float32)
            o = o.astype(jnp.bfloat16).astype(jnp.float32)
            base = c * (cols // LANES * STRIDE)
            for j in range(cols // LANES):
                xf[pl.ds(base + j * STRIDE, m), :] = o[:, j * LANES:(j + 1) * LANES]

    @pl.loop(0, experts)
    def _(e):
        slot = lax.rem(e, 2)
        n_seg = (cnt[2 * e], cnt[2 * e + 1])
        both = n_seg[0] + n_seg[1]
        merged = both <= CAP

        @pl.when(e + 1 < experts)
        def _():
            in_copies(e + 1, 1 - slot, True)

        @pl.loop(0, jnp.where(merged, 1, 2))
        def _(p):
            n = jnp.where(merged, both, jnp.where(p == 0, n_seg[0], n_seg[1]))
            counts = [jnp.where(merged | (p == q), n_seg[q], 0) for q in range(2)]
            starts = (0, jnp.where(merged, n_seg[0], 0))

            for q in range(2):
                @pl.loop(0, (counts[q] + UNROLL - 1) // UNROLL)
                def _(g, q=q):
                    pair = (2 * e + q) * CAP + g * UNROLL
                    row = starts[q] + g * UNROLL
                    for i in range(UNROLL):
                        xf[pl.ds(row + i, chunks, stride=STRIDE), :] = x_v[tok[pair + i]].astype(jnp.float32)

            @pl.when(p == 0)
            def _():
                in_copies(e, slot, False)

            lo = 0
            for m in SIZES:
                @pl.when((n > lo) & (n <= m))
                def _(m=m):
                    ffn(m, slot)

                lo = m

            @pl.when(p == 0)
            def _():
                copy_w(w2v, w2_sem, w2a, w2b, e, False)

            lo = 0
            for m in SIZES:
                @pl.when((n > lo) & (n <= m))
                def _(m=m):
                    down(m)

                lo = m

            @pl.when((e + 1 < experts) & (merged | (p == 1)))
            def _():
                copy_w(w2v, w2_sem, w2a, w2b, e + 1, True)

            for q in range(2):
                @pl.loop(0, (counts[q] + UNROLL - 1) // UNROLL)
                def _(g, q=q):
                    pair = (2 * e + q) * CAP + g * UNROLL
                    first = starts[q] + g * UNROLL
                    for b in range(0, UNROLL, BATCH):
                        sums = []
                        for i in range(b, b + BATCH):
                            base = pl.multiple_of(tok[pair + i] * chunks, chunks)
                            row = xf[pl.ds(first + i, chunks, stride=STRIDE), :]
                            sums.append((base, acc[pl.ds(base, chunks), :] + gate[pair + i] * row))
                        for base, val in sums:
                            acc[pl.ds(base, chunks), :] = val

    blk = stage.shape[1]
    n_out = half // blk
    for k, out_hbm in enumerate((outa_hbm, outb_hbm)):
        @pl.loop(0, n_out)
        def _(i, k=k, out_hbm=out_hbm):
            slot = lax.rem(i, 2)
            rows = pl.ds(pl.multiple_of(i * blk, blk), blk)

            @pl.when(i >= 2)
            def _():
                pltpu.make_async_copy(stage.at[slot], out_hbm.at[rows], out_sem.at[slot]).wait()

            for j in range(chunks):
                v = acc[pl.ds((k * half + i * blk) * chunks + j, blk, stride=chunks), :]
                stage[slot, :, j * LANES:(j + 1) * LANES] = v.astype(stage.dtype)
            pltpu.make_async_copy(stage.at[slot], out_hbm.at[rows], out_sem.at[slot]).start()

        for i in range(n_out - 2, n_out):
            pltpu.make_async_copy(stage.at[i % 2], out_hbm.at[pl.ds(i * blk, blk)], out_sem.at[i % 2]).wait()


def expert_bank(tok, gate, cnt, x3, w_own, w_peer, out_dtype):
    half, chunks, _ = x3[0].shape
    tokens = 2 * half
    per_dev, width, ff = w_own[0].shape
    blk = 128
    anys = pl.BlockSpec(memory_space=pl.ANY)
    smem = pl.BlockSpec(memory_space=pltpu.SMEM)
    flops = 2 * per_dev * 200 * 6 * width * ff
    return pl.pallas_call(
        bank_kernel,
        out_shape=[jax.ShapeDtypeStruct((half, width), out_dtype)] * 2,
        in_specs=[smem] * 3 + [anys] * 8,
        out_specs=[anys] * 2,
        scratch_shapes=[
            pltpu.VMEM((tokens + 8, chunks, LANES), jnp.bfloat16),
            pltpu.VMEM(((tokens + 16) * chunks, LANES), jnp.float32),
            pltpu.VMEM((2, width, ff), jnp.bfloat16),
            pltpu.VMEM((2, width, ff), jnp.bfloat16),
            pltpu.VMEM((ff, width), jnp.bfloat16),
            pltpu.VMEM((chunks * STRIDE, LANES), jnp.float32),
            pltpu.VMEM((CAP, width), jnp.bfloat16),
            pltpu.VMEM((CAP, ff), jnp.bfloat16),
            pltpu.VMEM((2, blk, width), out_dtype),
            pltpu.SemaphoreType.DMA((2,)),
            pltpu.SemaphoreType.DMA((2,)),
            pltpu.SemaphoreType.DMA((2,)),
            pltpu.SemaphoreType.DMA,
            pltpu.SemaphoreType.DMA((2,)),
        ],
        compiler_params=pltpu.CompilerParams(vmem_limit_bytes=66_000_000),
        cost_estimate=pl.CostEstimate(flops=flops, bytes_accessed=6 * per_dev * width * ff * 2, transcendentals=0),
    )(tok.reshape(-1), gate.reshape(-1), cnt, *x3, *w_own, *w_peer)


def join_kernel(shared, *refs):
    out = refs[-1]
    sums = []
    for h in range(2):
        total = refs[h][...].astype(jnp.float32)
        for r in refs[2 + h:-1:2]:
            total = total + r[...].astype(jnp.float32)
        sums.append(total)
    for g in range(out.shape[0] // 16):
        pair = jnp.concatenate([t[g * 8:g * 8 + 8] for t in sums], axis=0)
        out[g * 16:g * 16 + 16, :] = (shared[g * 16:g * 16 + 16, :] + pair).astype(out.dtype)


def join(shared, parts):
    tokens, width = shared.shape
    blk = 128
    half_spec = pl.BlockSpec((blk // 2, width), lambda i: (i, 0))
    full_spec = pl.BlockSpec((blk, width), lambda i: (i, 0))
    return pl.pallas_call(
        join_kernel,
        out_shape=jax.ShapeDtypeStruct((tokens, width), jnp.bfloat16),
        grid=(tokens // blk,),
        in_specs=[full_spec] + [half_spec] * len(parts),
        out_specs=full_spec,
        cost_estimate=pl.CostEstimate(flops=8 * tokens * width, bytes_accessed=14 * tokens * width, transcendentals=0),
    )(shared, *parts)


def solution(mesh):
    groups = mesh.shape["ep"]
    tok_spec = P(("dp", "ep"), None)
    bank_spec = P("ep", None, None)

    def swap(a, s):
        return lax.ppermute(a, "ep", [(i, i ^ s) for i in range(groups)])

    def device_fn(hidden, w_router, w_gate, w_up, w_down, shared_gate, shared_up, shared_down, top_idx, keep_mask):
        tokens, _ = top_idx.shape
        width = hidden.shape[1]
        experts = w_router.shape[1]
        per_chip = 2 * w_gate.shape[0]
        me = lax.axis_index("ep")
        rows = tokens // 2

        def halves(a):
            tiles = a.reshape(tokens // 16, 2, 8, a.shape[1])
            return tuple(tiles[:, h].reshape(rows, a.shape[1]) for h in range(2))

        x0 = tuple(h.reshape(rows, width // LANES, LANES) for h in halves(hidden))
        x2, x4 = (tuple(swap(h, s) for h in x0) for s in (2, 4))
        w_own = (w_gate, w_up, w_down)
        w_peer = tuple(swap(w, 1) for w in w_own)

        logits = jnp.dot(hidden, w_router, preferred_element_type=jnp.float32)
        prob = ROUTE_SCALE * jax.nn.softmax(logits, axis=-1)
        kept_id = jnp.where(keep_mask > 0, top_idx, experts)
        member = jnp.any(kept_id[:, :, None] == jnp.arange(experts)[None, None, :], axis=1)
        prob = jnp.concatenate(halves(prob), axis=1)
        member = jnp.concatenate(halves(member.astype(jnp.bfloat16)), axis=1)
        t_ids = jnp.arange(rows, dtype=jnp.int32)
        before = (t_ids[:, None] > t_ids[None, :]).astype(jnp.bfloat16)
        rank = jnp.dot(before, member, preferred_element_type=jnp.float32).astype(jnp.int32)
        rank = jnp.where(member > 0, rank, -1)
        hit = rank[:, :, None] == jnp.arange(CAP, dtype=jnp.int32)[None, None, :]
        slot_tok = jnp.min(jnp.where(hit, t_ids[:, None, None].astype(jnp.float32), float(rows)), axis=0)
        slot_gate = jnp.sum(jnp.where(hit, prob[:, :, None], 0.0), axis=0)
        lists = jnp.stack([slot_tok, slot_gate], axis=1).reshape(2, experts, 2, CAP)

        def lists_of(dev):
            return lax.dynamic_slice_in_dim(lists, (dev // 2) * per_chip, per_chip, axis=1)

        def run(xs, lst, out_dtype):
            half = per_chip // 2
            lst = jnp.stack(lst, axis=1)
            lst = jnp.where(lax.rem(me, 2) == 0, lst, jnp.concatenate([lst[half:], lst[:half]], axis=0))
            tok = lst[:, :, 0].astype(jnp.int32)
            used = tok < rows
            cnt = jnp.sum(used.astype(jnp.int32), axis=2).reshape(-1)
            tok = jnp.where(used, tok + jnp.array([0, rows], jnp.int32)[None, :, None], tokens)
            return expert_bank(tok, lst[:, :, 1], cnt, xs, w_own, w_peer, out_dtype)

        l_in = {s: swap(lists_of(me ^ s), s) for s in (2, 4, 6)}
        shared = swiglu(hidden, shared_gate, shared_up, shared_down)
        x2, x4, shared, l_in = lax.optimization_barrier((x2, x4, shared, l_in))
        x6 = swap(x4[0], 2), swap(x2[1], 4)
        a2, a4 = run((x2[0], x4[0]), (l_in[2][0], l_in[4][0]), jnp.bfloat16)
        back_a = swap(a2, 2), swap(a4, 4)
        x6, a2 = lax.optimization_barrier((x6, a2))
        b0, b1 = run(x6, (l_in[6][0], l_in[6][1]), jnp.bfloat16)
        back_b = swap(b0, 6), swap(b1, 6)
        c2, c4 = run((x2[1], x4[1]), (l_in[2][1], l_in[4][1]), jnp.bfloat16)
        back_c = swap(c2, 2), swap(c4, 4)
        mine = lists_of(me)
        own = run(x0, (mine[0], mine[1]), jnp.bfloat16)
        parts = [*own, *back_b, back_a[0], back_c[0], back_a[1], back_c[1]]
        return join(shared, parts)

    return jax.shard_map(device_fn, mesh=mesh, in_specs=(tok_spec, P(), bank_spec, bank_spec, bank_spec, P(), P(), P(), tok_spec, tok_spec), out_specs=tok_spec, check_vma=False)
```

time: 899 us -> 1050 us (1.17)
  waiting for transfers between devices: 227 us -> 365 us
  Pallas kernels: 441 us -> 487 us
  other arithmetic: 72.3 us -> 46.5 us
    ppermute x15 -> x18, waiting for transfers between devices: 227 us -> 365 us  [swap(): return lax.ppermute(a, 'ep', [(i, i ^ s) for i in range(groups)])]
    pallas_call x4 -> x5, Pallas kernels: 441 us -> 487 us  [the longest x4 464 us: expert_bank(): pl.pallas_call(bank_kernel, out_shape=[jax.ShapeDtypeStruct((half, width)...]
    add x1 -> x0, other arithmetic: 17 us -> none  [device_fn(): total = total + b.astype(jnp.float32)]
  transfers between devices with their start and end apart: 15 -> 18, of which waited for: 3 -> 6; matrix products, arithmetic and copies ran while one was open for 21% -> 16% of each run, Pallas kernels for 50% -> 44%
where the time goes in v2:
time: 1050 us; the launch traced here: 1040 us
  Pallas kernels  487 us (46%)
  waiting for transfers between devices  365 us (35%)
  matrix products  100 us (10%)
  other arithmetic  46.5 us (4%)
  local copies, waits for them, and re-layouts  24.7 us (2%)
  starting transfers between devices  20.3 us (2%)
    pallas_call x4, Pallas kernels, expert_bank(): pl.pallas_call(bank_kernel, out_shape=[jax.ShapeDtypeStruct((half, width)...  464 us
    ppermute x18, waiting for transfers between devices, swap(): return lax.ppermute(a, 'ep', [(i, i ^ s) for i in range(groups)])  365 us
    reduce_sum x1, other arithmetic, device_fn(): slot_gate = jnp.sum(jnp.where(hit, prob[:, :, None], 0.0), axis=0)  42.7 us
    dot_general x1, matrix products, swiglu(): h_up = jnp.dot(tok_rows, up_w, preferred_element_type=jnp.float32)  34.7 us
    dot_general x1, matrix products, swiglu(): return jnp.dot(act_rows, down_w, preferred_element_type=jnp.float32)  31.9 us
    dot_general x1, matrix products, swiglu(): h_gate = jnp.dot(tok_rows, gate_w, preferred_element_type=jnp.float32)  26.9 us
    pallas_call x1, Pallas kernels, join(): pl.pallas_call(join_kernel, out_shape=jax.ShapeDtypeStruct((tokens, width...  22.4 us
  transfers between devices with their start and end apart: 18, of which 6 were waited for; matrix products, arithmetic and copies ran while one was open for 16% of the time, Pallas kernels for 44%

profile of v2, /device:TPU:4, one launch (start us, length us, event | category | flops | bytes accessed | tf_op | source)
XLA Modules:
  0.0 1044.5 jit_solution(17285234409716575710)
XLA Ops:
  0.0 0.5 collective-permute-start.8
  0.6 0.4 copy-done
  1.0 6.0 fusion.32
  7.6 0.5 fusion.2
  8.8 0.8 fusion.4
  9.6 42.7 %select_reduce_fusion = (f32[128,384]{1,0:T(8,128)S(1)}, f32[128,384]{1,0:T(8,128)S(1)}) fusion(f32[1024,128]{1,0:T(8,128)S(1)} %pad_maximum_fusion, s32[1024,128]{1,0:T(8,128)S(1)} %fusion.4, f32[1024]{0:T(1024)S(1)} %iota_convert_fusion), kind=kLoop, calls=%fused_computation | loop fusion | flops 251559936 | bytes 1445888 | tf_op jit(solution)/shard_map/reduce_sum | solution.py:276
  52.3 1.5 collective-permute-start.4
  53.9 0.5 collective-permute-start.5
  54.4 3.9 slice_bitcast_fusion
  58.3 3.5 copy.76
  61.9 3.5 copy.77
  65.5 1.3 slice-done.1
  66.8 26.9 %fusion.33 = f32[2048,2816]{1,0:T(8,128)} fusion(bf16[2048,2048]{1,0:T(8,128)(2,1)S(1)} %bitcast.82, bf16[2048,2816]{1,0:T(8,128)(2,1)S(1)} %bitcast.94), kind=kOutput, calls=%fused_computation.100 | convolution fusion | flops 23622320128 | bytes 42991616 | tf_op jit(solution)/shard_map/dot_general | solution.py:18
  93.8 0.7 add.70
  94.5 0.6 copy-done.14
  95.1 1.5 collective-permute-start.6
  96.6 0.6 fusion.24
  97.3 1.5 collective-permute-start
  98.8 2.9 collective-permute-done.6
  101.7 34.7 %multiply_convert_fusion.clone.4 = bf16[2048,2816]{1,0:T(8,128)(2,1)} fusion(f32[2048,2816]{1,0:T(8,128)} %fusion.33, bf16[2048,2048]{1,0:T(8,128)(2,1)} %param.14, bf16[2048,2816]{1,0:T(8,128)(2,1)} %param.20), kind=kOutput, calls=%fused_computation.3.clone.clone.clone.1 | convolution fusion | flops 23656923136 | bytes 54525952 | tf_op jit(solution)/shard_map/dot_general | solution.py:19
  136.5 55.3 %collective-permute-done.xa_hbm = bf16[1024,16,128]{2,1,0:T(8,128)(2,1)} collective-permute-done((bf16[1024,16,128]{2,1,0:T(8,128)(2,1)}, bf16[1024,16,128]{2,1,0:T(8,128)(2,1)}, u32[]{:S(2)}, u32[]{:S(2)}) %collective-permute-start) | collective-permute-done | bytes 4194336 | tf_op jit(solution)/shard_map/ppermute | solution.py:245
  191.8 0.5 collective-permute-start.2
  192.3 88.0 %collective-permute-done.1.xa_hbm = bf16[1024,16,128]{2,1,0:T(8,128)(2,1)} collective-permute-done((bf16[1024,16,128]{2,1,0:T(8,128)(2,1)}, bf16[1024,16,128]{2,1,0:T(8,128)(2,1)}, u32[]{:S(2)}, u32[]{:S(2)}) %collective-permute-start.1) | collective-permute-done | bytes 4194336 | tf_op jit(solution)/shard_map/ppermute | solution.py:245
  280.3 0.4 collective-permute-start.3
  280.7 31.9 %fusion.shared = f32[2048,2048]{1,0:T(8,128)} fusion(bf16[2816,2048]{1,0:T(8,128)(2,1)} %param.21, bf16[2048,2816]{1,0:T(8,128)(2,1)} %multiply_convert_fusion.clone.4), kind=kOutput, calls=%fused_computation.4 | convolution fusion | flops 23622320128 | bytes 39845888 | tf_op jit(solution)/shard_map/dot_general | solution.py:21
  312.6 2.1 copy-done.3
  314.7 57.0 %collective-permute-done.3.xb_hbm = bf16[1024,16,128]{2,1,0:T(8,128)(2,1)S(1)} collective-permute-done((bf16[1024,16,128]{2,1,0:T(8,128)(2,1)}, bf16[1024,16,128]{2,1,0:T(8,128)(2,1)S(1)}, u32[]{:S(2)}, u32[]{:S(2)}) %collective-permute-start.3) | collective-permute-done | bytes 4194336 | tf_op jit(solution)/shard_map/ppermute | solution.py:245
  371.7 2.0 copy-done.4
  374.8 0.7 reshape_squeeze.31.gate
  375.4 0.4 fusion.17
  375.8 0.7 reshape.78.cnt
  376.5 0.7 reshape_squeeze.30.gate
  377.5 0.6 reshape.77.cnt
  378.1 0.9 collective-permute-start.10
  379.3 0.7 reshape_squeeze.29.gate
  380.2 0.6 reshape.76.cnt
  380.8 0.7 reshape_squeeze.28.gate
  381.6 0.7 reshape.75.cnt
  382.3 0.7 add_select_fusion
  383.0 109.7 %shard_map.139 = (bf16[1024,2048]{1,0:T(8,128)(2,1)}, bf16[1024,2048]{1,0:T(8,128)(2,1)}) custom-call(s32[12288]{0:T(1024)} %get-tuple-element.77.tok, f32[12288]{0:T(1024)} %reshape_squeeze.31.gate, s32[32]{0:T(128)} %reshape.78.cnt, bf16[1024,16,128]{2,1,0:T(8,128)(2,1)} %collective-permute-done.1.xa_hbm, bf16[1024,16,128]{2,1,0:T(8,128)(2,1)} %copy-done.4, ...), custom_call_target="tpu_custom_call" | custom-call | flops 55364812800 | bytes 276824064 | tf_op jit(solution)/shard_map/pallas_call | solution.py:185
  492.8 7.4 collective-permute-start.17
  500.2 128.1 %shard_map.137 = (bf16[1024,2048]{1,0:T(8,128)(2,1)}, bf16[1024,2048]{1,0:T(8,128)(2,1)}) custom-call(s32[12288]{0:T(1024)} %get-tuple-element.78.tok, f32[12288]{0:T(1024)} %reshape_squeeze.30.gate, s32[32]{0:T(128)} %reshape.77.cnt, bf16[1024,16,128]{2,1,0:T(8,128)(2,1)} %collective-permute-done.xa_hbm, bf16[1024,16,128]{2,1,0:T(8,128)(2,1)} %copy-done.3, ...), custom_call_target="tpu_custom_call" | custom-call | flops 55364812800 | bytes 276824064 | tf_op jit(solution)/shard_map/pallas_call | solution.py:185
  628.4 117.0 %shard_map.138 = (bf16[1024,2048]{1,0:T(8,128)(2,1)}, bf16[1024,2048]{1,0:T(8,128)(2,1)}) custom-call(s32[12288]{0:T(1024)} %get-tuple-element.79.tok, f32[12288]{0:T(1024)} %reshape_squeeze.29.gate, s32[32]{0:T(128)} %reshape.76.cnt, bf16[1024,16,128]{2,1,0:T(8,128)(2,1)} %collective-permute-done.10.xa_hbm, ...), custom_call_target="tpu_custom_call" | custom-call | flops 55364812800 | bytes 276824064 | tf_op jit(solution)/shard_map/pallas_call | solution.py:185
  745.4 5.1 collective-permute-start.12
  750.5 109.5 %shard_map.136 = (bf16[1024,2048]{1,0:T(8,128)(2,1)}, bf16[1024,2048]{1,0:T(8,128)(2,1)}) custom-call(s32[12288]{0:T(1024)} %get-tuple-element.80.tok, f32[12288]{0:T(1024)} %reshape_squeeze.28.gate, s32[32]{0:T(128)} %reshape.75.cnt, bf16[1024,16,128]{2,1,0:T(8,128)(2,1)} %bitcast.84, bf16[1024,16,128]{2,1,0:T(8,128)(2,1)} %bitcast.88, ...), custom_call_target="tpu_custom_call" | custom-call | flops 55364812800 | bytes 276824064 | tf_op jit(solution)/shard_map/pallas_call | solution.py:185
  860.0 62.7 %collective-permute-done.13.refs_3_ = bf16[1024,2048]{1,0:T(8,128)(2,1)} collective-permute-done((bf16[1024,2048]{1,0:T(8,128)(2,1)}, bf16[1024,2048]{1,0:T(8,128)(2,1)}, u32[]{:S(2)}, u32[]{:S(2)}) %collective-permute-start.13) | collective-permute-done | bytes 4194336 | tf_op jit(solution)/shard_map/ppermute | solution.py:245
  922.7 99.1 %collective-permute-done.16.refs_6_ = bf16[1024,2048]{1,0:T(8,128)(2,1)} collective-permute-done((bf16[1024,2048]{1,0:T(8,128)(2,1)}, bf16[1024,2048]{1,0:T(8,128)(2,1)}, u32[]{:S(2)}, u32[]{:S(2)}) %collective-permute-start.16) | collective-permute-done | bytes 4194336 | tf_op jit(solution)/shard_map/ppermute | solution.py:245
  1021.8 22.4 %shard_map.140 = bf16[2048,2048]{1,0:T(8,128)(2,1)} custom-call(f32[2048,2048]{1,0:T(8,128)} %fusion.shared, bf16[1024,2048]{1,0:T(8,128)(2,1)} %get-tuple-element.24.refs_0_, bf16[1024,2048]{1,0:T(8,128)(2,1)} %get-tuple-element.25.refs_1_, bf16[1024,2048]{1,0:T(8,128)(2,1)} %collective-permute-done.12.refs_2_, ...), custom_call_target="tpu_custom_call" | custom-call | flops 33554432 | bytes 58720256 | tf_op jit(solution)/shard_map/pallas_call | solution.py:229
  (110 shorter events, 3.5 us)
Async XLA Ops:
  0.0 1.0 copy-start
  0.0 7.5 copy-start.18
  0.0 7.5 copy-start.19
  0.0 383.0 %collective-permute-start.7 = (bf16[8,2048,1408]{2,1,0:T(8,128)(2,1)}, bf16[8,2048,1408]{2,1,0:T(8,128)(2,1)}, u32[]{:S(2)}, u32[]{:S(2)}) collective-permute-start(bf16[8,2048,1408]{2,1,0:T(8,128)(2,1)} %w1a.7), channel_id=1, source_target_pairs={{0,1},{1,0},{2,3},{3,2},{4,5},{5,4},{6,7},{7,6}} | collective-permute-start | bytes 138412032 | tf_op jit(solution)/shard_map/ppermute | solution.py:245
  0.0 383.0 %collective-permute-start.8 = (bf16[8,2048,1408]{2,1,0:T(8,128)(2,1)}, bf16[8,2048,1408]{2,1,0:T(8,128)(2,1)}, u32[]{:S(2)}, u32[]{:S(2)}) collective-permute-start(bf16[8,2048,1408]{2,1,0:T(8,128)(2,1)} %w3a.7), channel_id=1, source_target_pairs={{0,1},{1,0},{2,3},{3,2},{4,5},{5,4},{6,7},{7,6}} | collective-permute-start | bytes 138412032 | tf_op jit(solution)/shard_map/ppermute | solution.py:245
  0.5 382.5 %collective-permute-start.9 = (bf16[8,1408,2048]{2,1,0:T(8,128)(2,1)}, bf16[8,1408,2048]{2,1,0:T(8,128)(2,1)}, u32[]{:S(2)}, u32[]{:S(2)}) collective-permute-start(bf16[8,1408,2048]{2,1,0:T(8,128)(2,1)} %w2a.7), channel_id=1, source_target_pairs={{0,1},{1,0},{2,3},{3,2},{4,5},{5,4},{6,7},{7,6}} | collective-permute-start | bytes 138412032 | tf_op jit(solution)/shard_map/ppermute | solution.py:245
  52.3 42.2 %collective-permute-start.4 = (f32[2,16,2,384]{3,1,2,0:T(8,128)S(1)}, f32[2,16,2,384]{3,1,2,0:T(8,128)S(1)}, u32[]{:S(2)}, u32[]{:S(2)}) collective-permute-start(f32[2,16,2,384]{3,1,2,0:T(8,128)S(1)} %get-tuple-element.50), channel_id=1, source_target_pairs={{0,2},{1,3},{2,0},{3,1},{4,6},{5,7},{6,4},{7,5}} | collective-permute-start | bytes 294920 | tf_op jit(solution)/shard_map/ppermute | solution.py:245
  53.9 43.4 %collective-permute-start.5 = (f32[2,16,2,384]{3,1,2,0:T(8,128)S(1)}, f32[2,16,2,384]{3,1,2,0:T(8,128)S(1)}, u32[]{:S(2)}, u32[]{:S(2)}) collective-permute-start(f32[2,16,2,384]{3,1,2,0:T(8,128)S(1)} %get-tuple-element.51), channel_id=1, source_target_pairs={{0,4},{1,5},{2,6},{3,7},{4,0},{5,1},{6,2},{7,3}} | collective-permute-start | bytes 294920 | tf_op jit(solution)/shard_map/ppermute | solution.py:245
  54.4 11.1 %slice-start.2 = ((s8[11534336]{0:T(1024)(128)(4,1)}), s8[4194304]{0:T(1024)(128)(4,1)S(1)}, s32[]{:S(2)}) async-start(s8[11534336]{0:T(1024)(128)(4,1)} %bitcast.93), calls=%async_computation.2 | async-start | bytes 8388608
  54.4 11.1 %slice-start.3 = ((s8[11534336]{0:T(1024)(128)(4,1)}), s8[4194304]{0:T(1024)(128)(4,1)S(1)}, s32[]{:S(2)}) async-start(s8[11534336]{0:T(1024)(128)(4,1)} %bitcast.93), calls=%async_computation.3 | async-start | bytes 8388608
  58.3 7.1 slice-start
  58.3 7.1 slice-start.4
  61.9 4.9 slice-start.1
  66.8 29.8 %copy-start.5 = (f32[16,1,2,384]{3,0,2,1:T(8,128)}, f32[16,1,2,384]{3,0,2,1:T(8,128)S(1)}, u32[]{:S(2)}) copy-start(f32[16,1,2,384]{3,0,2,1:T(8,128)S(1)} %get-tuple-element.75) | copy-start | bytes 147460
  66.8 29.8 %copy-start.7 = (f32[16,1,2,384]{3,0,2,1:T(8,128)}, f32[16,1,2,384]{3,0,2,1:T(8,128)S(1)}, u32[]{:S(2)}) copy-start(f32[16,1,2,384]{3,0,2,1:T(8,128)S(1)} %get-tuple-element.76) | copy-start | bytes 147460
  94.5 0.6 copy-start.14
  95.1 6.6 collective-permute-start.6
  97.3 4.4 copy-start.16
  97.3 94.5 %collective-permute-start = (bf16[1024,16,128]{2,1,0:T(8,128)(2,1)}, bf16[1024,16,128]{2,1,0:T(8,128)(2,1)}, u32[]{:S(2)}, u32[]{:S(2)}) collective-permute-start(bf16[1024,16,128]{2,1,0:T(8,128)(2,1)} %bitcast.83), channel_id=1, source_target_pairs={{0,2},{1,3},{2,0},{3,1},{4,6},{5,7},{6,4},{7,5}} | collective-permute-start | bytes 12582920 | tf_op jit(solution)/shard_map/ppermute | solution.py:245
  101.7 34.7 %copy-start.12 = (f32[2,16,2,384]{3,1,2,0:T(8,128)}, f32[2,16,2,384]{3,1,2,0:T(8,128)S(1)}, u32[]{:S(2)}) copy-start(f32[2,16,2,384]{3,1,2,0:T(8,128)S(1)} %collective-permute-done.6) | copy-start | bytes 294916
  101.7 90.0 %copy-start.2 = (bf16[128,8,16,128]{3,2,1,0:T(8,128)(2,1)S(1)}, bf16[128,8,16,128]{3,2,1,0:T(8,128)(2,1)}, u32[]{:S(2)}) copy-start(bf16[128,8,16,128]{3,2,1,0:T(8,128)(2,1)} %copy.76) | copy-start | bytes 12582916
  101.7 178.6 %collective-permute-start.1 = (bf16[1024,16,128]{2,1,0:T(8,128)(2,1)}, bf16[1024,16,128]{2,1,0:T(8,128)(2,1)}, u32[]{:S(2)}, u32[]{:S(2)}) collective-permute-start(bf16[1024,16,128]{2,1,0:T(8,128)(2,1)} %bitcast.86), channel_id=1, source_target_pairs={{0,2},{1,3},{2,0},{3,1},{4,6},{5,7},{6,4},{7,5}} | collective-permute-start | bytes 12582920 | tf_op jit(solution)/shard_map/ppermute | solution.py:245
  136.4 237.3 %copy-start.6 = (f32[16,1,2,384]{3,0,2,1:T(8,128)S(1)}, f32[16,1,2,384]{3,0,2,1:T(8,128)}, u32[]{:S(2)}) copy-start(f32[16,1,2,384]{3,0,2,1:T(8,128)} %copy-done.5) | copy-start | bytes 147460
  136.4 237.3 %copy-start.8 = (f32[16,1,2,384]{3,0,2,1:T(8,128)S(1)}, f32[16,1,2,384]{3,0,2,1:T(8,128)}, u32[]{:S(2)}) copy-start(f32[16,1,2,384]{3,0,2,1:T(8,128)} %copy-done.7) | copy-start | bytes 147460
  136.4 237.3 %copy-start.10 = (f32[8,2,2,384]{3,0,2,1:T(8,128)S(1)}, f32[8,2,2,384]{3,0,2,1:T(8,128)}, u32[]{:S(2)}) copy-start(f32[8,2,2,384]{3,0,2,1:T(8,128)} %get-tuple-element.73) | copy-start | bytes 147460
  136.4 237.3 %copy-start.11 = (f32[8,2,2,384]{3,0,2,1:T(8,128)S(1)}, f32[8,2,2,384]{3,0,2,1:T(8,128)}, u32[]{:S(2)}) copy-start(f32[8,2,2,384]{3,0,2,1:T(8,128)} %get-tuple-element.74) | copy-start | bytes 147460
  136.5 237.6 %copy-start.15 = (f32[2,16,2,384]{3,1,2,0:T(8,128)S(1)}, f32[2,16,2,384]{3,1,2,0:T(8,128)}, u32[]{:S(2)}) copy-start(f32[2,16,2,384]{3,1,2,0:T(8,128)} %copy-done.14) | copy-start | bytes 294916
  136.5 237.6 %copy-start.17 = (f32[2,16,2,384]{3,1,2,0:T(8,128)S(1)}, f32[2,16,2,384]{3,1,2,0:T(8,128)}, u32[]{:S(2)}) copy-start(f32[2,16,2,384]{3,1,2,0:T(8,128)} %copy-done.16) | copy-start | bytes 294916
  136.5 245.8 %copy-start.9 = (s32[12288]{0:T(1024)S(1)}, s32[12288]{0:T(1024)}, u32[]{:S(2)}) copy-start(s32[12288]{0:T(1024)} %add.70) | copy-start | bytes 147460
  191.8 182.0 %copy-start.13 = (f32[2,16,2,384]{3,1,2,0:T(8,128)S(1)}, f32[2,16,2,384]{3,1,2,0:T(8,128)}, u32[]{:S(2)}) copy-start(f32[2,16,2,384]{3,1,2,0:T(8,128)} %copy-done.12) | copy-start | bytes 294916
  191.8 120.9 %collective-permute-start.2 = (bf16[1024,16,128]{2,1,0:T(8,128)(2,1)S(1)}, bf16[1024,16,128]{2,1,0:T(8,128)(2,1)S(1)}, u32[]{:S(2)}, u32[]{:S(2)}) collective-permute-start(bf16[1024,16,128]{2,1,0:T(8,128)(2,1)S(1)} %bitcast.85), channel_id=1, source_target_pairs={{0,4},{1,5},{2,6},{3,7},{4,0},{5,1},{6,2},{7,3}} | collective-permute-start | bytes 12582920 | tf_op jit(solution)/shard_map/ppermute | solution.py:245
  280.3 91.4 %collective-permute-start.3 = (bf16[1024,16,128]{2,1,0:T(8,128)(2,1)}, bf16[1024,16,128]{2,1,0:T(8,128)(2,1)S(1)}, u32[]{:S(2)}, u32[]{:S(2)}) collective-permute-start(bf16[1024,16,128]{2,1,0:T(8,128)(2,1)} %bitcast.87), channel_id=1, source_target_pairs={{0,4},{1,5},{2,6},{3,7},{4,0},{5,1},{6,2},{7,3}} | collective-permute-start | bytes 12582920 | tf_op jit(solution)/shard_map/ppermute | solution.py:245
  312.6 2.1 copy-start.3
  371.7 2.0 copy-start.4
  378.1 250.3 %collective-permute-start.10 = (bf16[1024,16,128]{2,1,0:T(8,128)(2,1)}, bf16[1024,16,128]{2,1,0:T(8,128)(2,1)}, u32[]{:S(2)}, u32[]{:S(2)}) collective-permute-start(bf16[1024,16,128]{2,1,0:T(8,128)(2,1)} %copy-done.3), channel_id=1, source_target_pairs={{0,2},{1,3},{2,0},{3,1},{4,6},{5,7},{6,4},{7,5}} | collective-permute-start | bytes 12582920 | tf_op jit(solution)/shard_map/ppermute | solution.py:245
  379.0 249.4 %collective-permute-start.11 = (bf16[1024,16,128]{2,1,0:T(8,128)(2,1)}, bf16[1024,16,128]{2,1,0:T(8,128)(2,1)}, u32[]{:S(2)}, u32[]{:S(2)}) collective-permute-start(bf16[1024,16,128]{2,1,0:T(8,128)(2,1)} %collective-permute-done.1.xa_hbm), channel_id=1, source_target_pairs={{0,4},{1,5},{2,6},{3,7},{4,0},{5,1},{6,2},{7,3}} | collective-permute-start | bytes 12582920 | tf_op jit(solution)/shard_map/ppermute | solution.py:245
  492.8 257.7 %collective-permute-start.15 = (bf16[1024,2048]{1,0:T(8,128)(2,1)}, bf16[1024,2048]{1,0:T(8,128)(2,1)}, u32[]{:S(2)}, u32[]{:S(2)}) collective-permute-start(bf16[1024,2048]{1,0:T(8,128)(2,1)} %get-tuple-element.38), channel_id=1, source_target_pairs={{0,2},{1,3},{2,0},{3,1},{4,6},{5,7},{6,4},{7,5}} | collective-permute-start | bytes 12582920 | tf_op jit(solution)/shard_map/ppermute | solution.py:245
  492.8 367.2 %collective-permute-start.17 = (bf16[1024,2048]{1,0:T(8,128)(2,1)}, bf16[1024,2048]{1,0:T(8,128)(2,1)}, u32[]{:S(2)}, u32[]{:S(2)}) collective-permute-start(bf16[1024,2048]{1,0:T(8,128)(2,1)} %get-tuple-element.40), channel_id=1, source_target_pairs={{0,4},{1,5},{2,6},{3,7},{4,0},{5,1},{6,2},{7,3}} | collective-permute-start | bytes 12582920 | tf_op jit(solution)/shard_map/ppermute | solution.py:245
  628.3 294.4 %collective-permute-start.14 = (bf16[1024,2048]{1,0:T(8,128)(2,1)}, bf16[1024,2048]{1,0:T(8,128)(2,1)}, u32[]{:S(2)}, u32[]{:S(2)}) collective-permute-start(bf16[1024,2048]{1,0:T(8,128)(2,1)} %get-tuple-element.32), channel_id=1, source_target_pairs={{0,2},{1,3},{2,0},{3,1},{4,6},{5,7},{6,4},{7,5}} | collective-permute-start | bytes 12582920 | tf_op jit(solution)/shard_map/ppermute | solution.py:245
  745.4 114.6 %collective-permute-start.12 = (bf16[1024,2048]{1,0:T(8,128)(2,1)}, bf16[1024,2048]{1,0:T(8,128)(2,1)}, u32[]{:S(2)}, u32[]{:S(2)}) collective-permute-start(bf16[1024,2048]{1,0:T(8,128)(2,1)} %get-tuple-element.35), channel_id=1, source_target_pairs={{0,6},{1,7},{2,4},{3,5},{4,2},{5,3},{6,0},{7,1}} | collective-permute-start | bytes 12582920 | tf_op jit(solution)/shard_map/ppermute | solution.py:245
  750.4 172.3 %collective-permute-start.13 = (bf16[1024,2048]{1,0:T(8,128)(2,1)}, bf16[1024,2048]{1,0:T(8,128)(2,1)}, u32[]{:S(2)}, u32[]{:S(2)}) collective-permute-start(bf16[1024,2048]{1,0:T(8,128)(2,1)} %get-tuple-element.36), channel_id=1, source_target_pairs={{0,6},{1,7},{2,4},{3,5},{4,2},{5,3},{6,0},{7,1}} | collective-permute-start | bytes 12582920 | tf_op jit(solution)/shard_map/ppermute | solution.py:245
  750.5 271.4 %collective-permute-start.16 = (bf16[1024,2048]{1,0:T(8,128)(2,1)}, bf16[1024,2048]{1,0:T(8,128)(2,1)}, u32[]{:S(2)}, u32[]{:S(2)}) collective-permute-start(bf16[1024,2048]{1,0:T(8,128)(2,1)} %get-tuple-element.39), channel_id=1, source_target_pairs={{0,4},{1,5},{2,6},{3,7},{4,0},{5,1},{6,2},{7,3}} | collective-permute-start | bytes 12582920 | tf_op jit(solution)/shard_map/ppermute | solution.py:245
  1021.8 22.4 %copy-start.1 = (bf16[2048,64]{0,1:T(8,128)(2,1)S(1)}, bf16[2048,64]{0,1:T(8,128)(2,1)}, u32[]{:S(2)}) copy-start(bf16[2048,64]{0,1:T(8,128)(2,1)} %param.15) | copy-start | bytes 786436
